TPU v7x, 32 devices: a whole 2x2x4 slice. The times are simulated.
32 devices in a mesh: dp: 32 (over z, y, x, core).
Axes of the slice: x: 2, y: 2, z: 4, core: 2. Of those that a mesh axis runs over, the one named last changes fastest.
Arguments:
- act_in: bfloat16 [2048, 7, 7, 2048], P('dp')
- shortcut: bfloat16 [2048, 7, 7, 2048], P('dp')
- labels: int32 [2048], P('dp')
- w_conv: float32 [2048, 2048], replicated
- bn_gamma: float32 [2048], replicated
- bn_beta: float32 [2048], replicated
- w_fc: float32 [2048, 1000], replicated
- fc_bias: float32 [1000], replicated
- vel_conv: float32 [2048, 2048], replicated
- vel_gamma: float32 [2048], replicated
- vel_beta: float32 [2048], replicated
- vel_fc: float32 [2048, 1000], replicated
- vel_bias: float32 [1000], replicated
- learn_rate: float32 [], replicated
Outputs:
- output 1: float32 [2048, 2048], replicated
- output 2: float32 [2048], replicated
- output 3: float32 [2048], replicated
- output 4: float32 [2048, 1000], replicated
- output 5: float32 [1000], replicated
- output 6: float32 [2048, 2048], replicated
- output 7: float32 [2048], replicated
- output 8: float32 [2048], replicated
- output 9: float32 [2048, 1000], replicated
- output 10: float32 [1000], replicated
- output 11: float32 [], replicated
All inputs are finite; a program needn't handle non-finite values.
Results may differ from a plain program's by a relative error of at most 0.00889668.
Values sent between devices are 32-bit elements.
A program may use at most 1 GiB of HBM per device.

v0:
```python
import jax
import jax.numpy as jnp
from jax import lax
from jax.sharding import PartitionSpec as P

BN_EPS = 1e-5
SMOOTHING = 0.1
MOMENTUM = 0.9
TRUST_COEF = 0.001
WEIGHT_DECAY = 5e-5


def forward_backward(act_in, shortcut, labels, w_conv, bn_gamma, bn_beta, w_fc, fc_bias, global_rows):
    per_dev = act_in.shape[0]
    spatial = act_in.shape[1] * act_in.shape[2]
    c_mid = act_in.shape[3]
    c_out = shortcut.shape[3]
    classes = w_fc.shape[1]
    pos_count = per_dev * spatial
    act_grid = act_in.reshape(per_dev, spatial, c_mid)
    conv_out = jnp.einsum('bpc,cd->bpd', act_grid, w_conv.astype(jnp.bfloat16), preferred_element_type=jnp.float32)
    batch_mean = jnp.mean(conv_out, axis=(0, 1))
    centered = conv_out - batch_mean
    inv_std = lax.rsqrt(jnp.mean(jnp.square(centered), axis=(0, 1)) + BN_EPS)
    x_hat = centered * inv_std
    pre_act = x_hat * bn_gamma + bn_beta + shortcut.reshape(per_dev, spatial, c_out).astype(jnp.float32)
    pooled = jnp.mean(jax.nn.relu(pre_act), axis=1)
    pooled_bf = pooled.astype(jnp.bfloat16)
    fc_bf = w_fc.astype(jnp.bfloat16)
    logits = jnp.dot(pooled_bf, fc_bf, preferred_element_type=jnp.float32) + fc_bias
    log_prob = jax.nn.log_softmax(logits, axis=-1)
    one_hot_lab = (labels[:, None] == jnp.arange(classes, dtype=jnp.int32)[None, :]).astype(jnp.float32)
    target = SMOOTHING / classes + (1.0 - SMOOTHING) * one_hot_lab
    loss_part = -jnp.sum(target * log_prob) / global_rows
    d_logits = (jnp.exp(log_prob) - target) / global_rows
    d_bias = jnp.sum(d_logits, axis=0)
    d_logits_bf = d_logits.astype(jnp.bfloat16)
    d_fc = jnp.einsum('bc,bk->ck', pooled_bf, d_logits_bf, preferred_element_type=jnp.float32)
    d_pool = jnp.einsum('bk,ck->bc', d_logits_bf, fc_bf, preferred_element_type=jnp.float32) / spatial
    d_pre = jnp.where(pre_act > 0, d_pool[:, None, :], 0.0)
    d_beta = jnp.sum(d_pre, axis=(0, 1))
    d_gamma = jnp.sum(d_pre * x_hat, axis=(0, 1))
    d_conv_out = (bn_gamma * inv_std) * (d_pre - d_beta / pos_count - x_hat * (d_gamma / pos_count))
    d_conv = jnp.einsum('bpc,bpd->cd', act_grid, d_conv_out.astype(jnp.bfloat16), preferred_element_type=jnp.float32)
    return d_conv, d_gamma, d_beta, d_fc, d_bias, loss_part


def lars_update(weight, gradient, velocity, learn_rate):
    w_norm = jnp.sqrt(jnp.sum(jnp.square(weight)))
    g_norm = jnp.sqrt(jnp.sum(jnp.square(gradient)))
    trust = TRUST_COEF * w_norm / (g_norm + WEIGHT_DECAY * w_norm)
    new_vel = MOMENTUM * velocity + learn_rate * trust * (gradient + WEIGHT_DECAY * weight)
    return weight - new_vel, new_vel


def solution(mesh):
    groups = mesh.shape['dp']

    def local_step(act_in, shortcut, labels, w_conv, bn_gamma, bn_beta, w_fc, fc_bias, vel_conv, vel_gamma, vel_beta, vel_fc, vel_bias, learn_rate):
        global_rows = act_in.shape[0] * groups
        local_terms = forward_backward(act_in, shortcut, labels, w_conv, bn_gamma, bn_beta, w_fc, fc_bias, global_rows)
        g_conv, g_gamma, g_beta, g_fc, g_bias, loss_val = lax.psum(local_terms, 'dp')
        conv_new, conv_vel_new = lars_update(w_conv, g_conv, vel_conv, learn_rate)
        fc_new, fc_vel_new = lars_update(w_fc, g_fc, vel_fc, learn_rate)
        gamma_vel_new = MOMENTUM * vel_gamma + learn_rate * g_gamma
        beta_vel_new = MOMENTUM * vel_beta + learn_rate * g_beta
        bias_vel_new = MOMENTUM * vel_bias + learn_rate * g_bias
        return (conv_new, bn_gamma - gamma_vel_new, bn_beta - beta_vel_new, fc_new, fc_bias - bias_vel_new, conv_vel_new, gamma_vel_new, beta_vel_new, fc_vel_new, bias_vel_new, loss_val)

    return jax.shard_map(local_step, mesh=mesh, in_specs=(P('dp'),) * 3 + (P(),) * 11, out_specs=(P(),) * 11, check_vma=False)
```

profile of v0, /device:TPU:0, one launch (start us, length us, event | category | flops | bytes accessed | tf_op | source)
XLA Modules:
  0.0 673.8 jit_solution(545843754179686269)
XLA Ops:
  7.2 36.1 %fusion.39 = (f32[2048]{0:T(1024)S(1)}, f32[64,49,2048]{2,0,1:T(8,128)}) fusion(bf16[64,49,2048]{2,0,1:T(8,128)(2,1)} %bitcast.22, f32[2048,2048]{1,0:T(8,128)} %param.17), kind=kOutput, calls=%fused_computation.60 | convolution fusion | flops 26317289472 | bytes 55320576 | tf_op jit(solution)/shard_map/bpc,cd->bpd/dot_general | solution.py:21
  43.4 10.0 %multiply_reduce_fusion = f32[2048]{0:T(1024)S(1)} fusion(f32[64,49,2048]{2,0,1:T(8,128)} %get-tuple-element.45, f32[2048]{0:T(1024)S(1)} %broadcast_multiply_fusion.2), kind=kLoop, calls=%fused_computation.9 | loop fusion | flops 19265536 | bytes 25706496 | tf_op jit(solution)/shard_map/reduce_sum | solution.py:24
  53.5 5.6 copy-done
  59.1 10.3 %maximum_reduce_fusion = f32[64,2048]{1,0:T(8,128)S(1)} fusion(bf16[64,7,7,2048]{3,0,2,1:T(8,128)(2,1)} %param.15, f32[2048]{0:T(1024)S(1)} %copy-done.2, f32[2048]{0:T(1024)S(1)} %copy-done.1, f32[2048]{0:T(1024)S(1)} %add_rsqrt_fusion, f32[64,49,2048]{2,0,1:T(8,128)S(1)} %copy-done, f32[2048]{0:T(1024)S(1)} %broadcast_multiply_fusion.2), kind=kLoop, calls=%fused_computation.8 | loop fusion | flops 51249152 | bytes 39092224 | tf_op jit(solution)/shard_map/reduce_sum | solution.py:27
  69.4 1.4 fusion.40
  71.1 4.7 fusion.27
  75.8 0.8 multiply_reduce_fusion.5
  76.6 1.0 convolution_multiply_fusion
  78.3 20.0 %select_reduce_fusion = (f32[2048]{0:T(1024)S(1)}, f32[2048]{0:T(1024)S(1)}, pred[64,49,2048]{2,0,1:T(32,128)(4,1)}) fusion(f32[64,2048]{1,0:T(8,128)S(1)} %convolution_multiply_fusion, f32[2048]{0:T(1024)S(1)} %add_rsqrt_fusion, f32[64,49,2048]{2,0,1:T(8,128)} %get-tuple-element.45, f32[2048]{0:T(1024)S(1)} %broadcast_multiply_fusion.2, ...), kind=kLoop, calls=%fused_computation.2 | loop fusion | flops 70643712 | bytes 45531136 | tf_op jit(solution)/shard_map/reduce_sum | solution.py:41
  99.0 42.6 %all-reduce = (f32[2048]{0:T(1024)S(1)}, f32[2048]{0:T(1024)S(1)}, f32[1000]{0:T(1024)S(1)}, f32[]{:T(128)}) all-reduce(f32[2048]{0:T(1024)S(1)} %get-tuple-element.23, f32[2048]{0:T(1024)S(1)} %get-tuple-element.22, f32[1000]{0:T(1024)S(1)} %get-tuple-element.25, f32[]{:T(128)S(6)} %div.43), channel_id=1, replica_groups=mesh['dp'=32] {'dp'}, use_global_device_ids=true, to_apply=%region_10.11 | all-reduce | flops 5097 | bytes 40776 | tf_op jit(solution)/shard_map/psum | solution.py:62
  141.6 0.6 fusion.37
  142.2 40.2 %fusion.13 = f32[2048,2048]{0,1:T(8,128)} fusion(bf16[64,49,2048]{2,0,1:T(8,128)(2,1)} %bitcast.23, pred[64,49,2048]{2,0,1:T(32,128)(4,1)} %get-tuple-element.42, f32[64,49,2048]{2,0,1:T(8,128)} %get-tuple-element.45, f32[2048]{0:T(1024)S(1)} %get-tuple-element.48, f32[2048]{0:T(1024)S(1)} %get-tuple-element.49, ...), kind=kOutput, calls=%fused_computation.23 | convolution fusion | flops 26358054912 | bytes 62300160 | tf_op jit(solution)/shard_map/bpc,bpd->cd/dot_general | solution.py:44
  182.4 6.0 multiply_reduce_fusion.4
  189.2 10.7 %multiply_reduce_fusion.2 = f32[]{:T(128)} fusion(f32[2048,2048]{1,0:T(8,128)} %param.17), kind=kLoop, calls=%fused_computation.13 | loop fusion | flops 8388607 | bytes 16777220 | tf_op jit(solution)/shard_map/reduce_sum | solution.py:49
  200.6 17.6 %copy.27 = f32[2048,2048]{0,1:T(8,128)} copy(f32[2048,2048]{1,0:T(8,128)} %param.17) | data formatting | bytes 33554432 | tf_op args[3]
  218.2 17.6 %copy.25 = f32[2048,2048]{0,1:T(8,128)} copy(f32[2048,2048]{1,0:T(8,128)} %param.22) | data formatting | bytes 33554432 | tf_op args[8]
  236.4 0.6 fusion.36
  237.0 335.4 %all-reduce.4.cloned.1.call-done = (f32[2048,2048]{0,1:T(8,128)}, f32[2048,1000]{0,1:T(8,128)}) async-done(((f32[2048,2048]{0,1:T(8,128)}, f32[2048,1000]{0,1:T(8,128)}), (f32[2048,2048]{0,1:T(8,128)}, f32[2048,1000]{0,1:T(8,128)})) %all-reduce.4.cloned.1.call-update) | async-done | bytes 24969232 | tf_op jit(solution)/shard_map/psum | solution.py:62
  572.4 6.0 multiply_reduce_fusion.3
  579.2 10.7 %multiply_reduce_fusion.1 = f32[]{:T(128)} fusion(f32[2048,2048]{0,1:T(8,128)} %get-tuple-element.30), kind=kLoop, calls=%fused_computation.12 | loop fusion | flops 8388607 | bytes 16777220 | tf_op jit(solution)/shard_map/reduce_sum | solution.py:50
  590.6 27.3 %fusion.38 = (f32[2048,2048]{0,1:T(8,128)}, f32[2048,2048]{0,1:T(8,128)}) fusion(f32[2048,2048]{0,1:T(8,128)} %copy.27, f32[2048,2048]{0,1:T(8,128)} %get-tuple-element.30, f32[]{:T(128)S(6)} %mul.145, f32[2048,2048]{0,1:T(8,128)} %copy.25), kind=kLoop, calls=%fused_computation.59 | loop fusion | flops 25165824 | bytes 83886080 | tf_op jit(solution)/shard_map/sub | solution.py:53
  617.9 17.6 %copy.28 = f32[2048,2048]{1,0:T(8,128)} copy(f32[2048,2048]{0,1:T(8,128)} %get-tuple-element.40) | data formatting | bytes 33554432
  635.5 17.6 %copy.29 = f32[2048,2048]{1,0:T(8,128)} copy(f32[2048,2048]{0,1:T(8,128)} %get-tuple-element.41) | data formatting | bytes 33554432
  653.1 13.9 %fusion.35 = (f32[2048,1000]{0,1:T(8,128)}, f32[2048,1000]{0,1:T(8,128)}) fusion(f32[2048,1000]{0,1:T(8,128)} %param.20, f32[2048,1000]{0,1:T(8,128)} %get-tuple-element.31, f32[]{:T(128)S(6)} %mul.159, f32[2048,1000]{0,1:T(8,128)} %param.25), kind=kLoop, calls=%fused_computation.56 | loop fusion | flops 12288000 | bytes 40960004 | tf_op jit(solution)/shard_map/sub | solution.py:53
  (28 shorter events, 0.9 us)
Async XLA Ops:
  7.2 565.2 %all-reduce.4.cloned.1.call-start = ((), (), s32[]{:S(2)}) async-start(), calls=%async_computation | async-start | bytes 49938432 | tf_op jit(solution)/shard_map/psum | solution.py:62
  43.4 15.7 %copy-start = (f32[64,49,2048]{2,0,1:T(8,128)S(1)}, f32[64,49,2048]{2,0,1:T(8,128)}, u32[]{:S(2)}) copy-start(f32[64,49,2048]{2,0,1:T(8,128)} %get-tuple-element.45) | copy-start | bytes 77070336
  43.4 15.7 %copy-start.1 = (f32[2048]{0:T(1024)S(1)}, f32[2048]{0:T(1024)}, u32[]{:S(2)}) copy-start(f32[2048]{0:T(1024)} %param.18) | copy-start | bytes 24580
  43.4 15.7 %copy-start.2 = (f32[2048]{0:T(1024)S(1)}, f32[2048]{0:T(1024)}, u32[]{:S(2)}) copy-start(f32[2048]{0:T(1024)} %param.19) | copy-start | bytes 24580
  43.4 26.0 %slice-start = ((s8[8192000]{0:T(1024)(128)(4,1)}), s8[4194304]{0:T(1024)(128)(4,1)S(1)}, s32[]{:S(2)}) async-start(s8[8192000]{0:T(1024)(128)(4,1)} %bitcast.20), calls=%async_computation.1 | async-start | bytes 8388608
  59.0 10.3 %slice-start.1 = ((s8[8192000]{0:T(1024)(128)(4,1)}), s8[3997696]{0:T(1024)(128)(4,1)S(1)}, s32[]{:S(2)}) async-start(s8[8192000]{0:T(1024)(128)(4,1)} %bitcast.20), calls=%async_computation.2 | async-start | bytes 7995392
  59.0 10.3 %copy-start.3 = (f32[1000]{0:T(1024)S(1)}, f32[1000]{0:T(1024)}, u32[]{:S(2)}) copy-start(f32[1000]{0:T(1024)} %param.21) | copy-start | bytes 12004
  59.1 12.0 %copy-start.6 = (s32[64]{0:T(128)S(1)}, s32[64]{0:T(128)}, u32[]{:S(2)}) copy-start(s32[64]{0:T(128)} %param.16) | copy-start | bytes 772
  78.3 63.3 %copy-start.4 = (f32[2048]{0:T(1024)S(1)}, f32[2048]{0:T(1024)}, u32[]{:S(2)}) copy-start(f32[2048]{0:T(1024)} %param.23) | copy-start | bytes 24580
  218.2 17.6 %copy-start.7 = (f32[1000]{0:T(1024)S(1)}, f32[1000]{0:T(1024)}, u32[]{:S(2)}) copy-start(f32[1000]{0:T(1024)} %param.26) | copy-start | bytes 12004
  218.2 18.2 %copy-start.5 = (f32[2048]{0:T(1024)S(1)}, f32[2048]{0:T(1024)}, u32[]{:S(2)}) copy-start(f32[2048]{0:T(1024)} %param.24) | copy-start | bytes 24580
Sparse Core Ops, SparseCore 0:
  182.6 389.7 all-reduce.3
where the time goes:
time: 675 us; the launch traced here: 674 us
  waiting for transfers between devices  335 us (50%)
  other arithmetic  118 us (17%)
  matrix products  83.5 us (12%)
  local copies, waits for them, and re-layouts  76 us (11%)
  blocking collectives  42.6 us (6%)
  between operations  18.3 us (3%)
    psum x1, waiting for transfers between devices, local_step(): lax.psum(local_terms, 'dp')  335 us
    unnamed x24, local copies, waits for them, and re-layouts  76 us
    psum x1, blocking collectives, local_step(): lax.psum(local_terms, 'dp')  42.6 us
    sub x2, other arithmetic, lars_update(): return (weight - new_vel, new_vel)  41.2 us
    dot_general x1, matrix products, forward_backward(): jnp.einsum('bpc,bpd->cd', act_grid, d_conv_out.astype(jnp.bfloat16), pref...  40.2 us
    dot_general x1, matrix products, forward_backward(): jnp.einsum('bpc,cd->bpd', act_grid, w_conv.astype(jnp.bfloat16), preferre...  36.1 us
    reduce_sum x1, other arithmetic, forward_backward(): d_beta = jnp.sum(d_pre, axis=(0, 1))  20 us
    reduce_sum x2, other arithmetic, lars_update(): w_norm = jnp.sqrt(jnp.sum(jnp.square(weight)))  16.7 us
  transfers between devices with their start and end apart: 1, of which 1 were waited for; matrix products, arithmetic and copies ran while one was open for 8% of the time, Pallas kernels for 0%

commit v1 on v0

v1 whole, which is shorter than its diff:
```python
import functools

import jax
import jax.numpy as jnp
from jax import lax
from jax.experimental import pallas as pl
from jax.experimental.pallas import tpu as pltpu
from jax.sharding import PartitionSpec as P

BN_EPS = 1e-5
SMOOTHING = 0.1
MOMENTUM = 0.9
TRUST_COEF = 0.001
WEIGHT_DECAY = 5e-5

F32 = jnp.float32
UR = 128
CS = 2
DEPTH = 3
ORDER = (3, 2, 1, 0, 7, 6, 5, 4)
MESH_ID = pl.DeviceIdType.MESH


def bytes_wait(ref, sem):
    pltpu.make_async_copy(ref, ref, sem).wait()


def reduce_kernel(n_dev, fc_rows, fc_units, n_units, gf_ref, gc_ref, of_ref, oc_ref, nrm_ref,
                  g, ba, bm, acc, ld, r0, r1, r2, r3, r4, r5, r6, r7, send, osem, credit):
    me = lax.axis_index('dp')
    core = me % 2
    zc = me // 8
    partner = me + 1 - 2 * core
    cols = g.shape[2]
    h, q, e = UR // 2, UR // 4, UR // 16
    mine = pl.ds(pl.multiple_of(core * UR, 8), UR)
    other = pl.ds(pl.multiple_of((1 - core) * UR, 8), UR)

    def rows(off, size):
        return pl.ds(pl.multiple_of(off, 8), size)

    def remote(src, dst, u, sem, dev):
        pltpu.make_async_remote_copy(src_ref=src, dst_ref=dst, send_sem=send.at[u], recv_sem=sem.at[u],
                                     device_id=(dev,), device_id_type=MESH_ID).start()

    def grant(k, u, dev):
        pl.semaphore_signal(credit.at[k, u], inc=1, device_id=(dev,), device_id_type=MESH_ID)

    class Place:
        def __init__(self, u):
            s_a = 2 + 2 * (u % 2)
            s_b = 6 - s_a
            bit_a = (me // s_a) % 2
            self.bit_b = (me // s_b) % 2
            self.dev_a = me + s_a * (1 - 2 * bit_a)
            self.dev_b = me + s_b * (1 - 2 * self.bit_b)
            self.keep_a = core * UR + bit_a * h
            self.give_a = core * UR + (1 - bit_a) * h
            self.quarter = self.keep_a + self.bit_b * q

    def z_peers():
        return [(d, (zc + d) % 4, (me + 8 * d) % n_dev) for d in (1, 3, 2)]

    barrier = pltpu.get_barrier_semaphore()

    def hello(d, c):
        pl.semaphore_signal(barrier, inc=1, device_id=((me + d) % n_dev,), device_id_type=MESH_ID)
        return c
    lax.fori_loop(1, n_dev, hello, 0)

    def hbm_slice(u, half):
        return rows((u // CS) * 2 * UR + half * UR, UR), pl.ds(pl.multiple_of((u % CS) * cols, 128), cols)

    def load_from(ref, first, last):
        def step(u, c):
            i, j = hbm_slice(u - first, core)
            pltpu.make_async_copy(ref.at[i, j], g.at[u, mine], ld.at[u]).start()
            return c
        lax.fori_loop(first, last, step, 0)

    def pair_from(ref, first, last):
        def step(u, c):
            i, j = hbm_slice(u - first, 1 - core)
            remote(ref.at[i, j], g.at[u, mine], u, r0, partner)
            return c
        lax.fori_loop(first, last, step, 0)

    load_from(gf_ref, 0, fc_units)
    load_from(gc_ref, fc_units, n_units)
    acc[...] = jnp.zeros_like(acc)
    pl.semaphore_wait(barrier, n_dev - 1)
    pair_from(gf_ref, 0, fc_units)
    pair_from(gc_ref, fc_units, n_units)

    def stage0(u):
        p = Place(u)
        bytes_wait(g.at[u, mine], ld.at[u])
        bytes_wait(g.at[u, mine], send.at[u])
        bytes_wait(g.at[u, other], r0.at[u])
        g[u, mine] += g[u, other]
        grant(0, u, partner)
        remote(g.at[u, rows(p.give_a, h)], ba.at[u], u, r1, p.dev_a)

    def stage1(u):
        p = Place(u)
        bytes_wait(ba.at[u], send.at[u])
        grant(1, u, p.dev_a)
        bytes_wait(ba.at[u], r1.at[u])
        g[u, rows(p.keep_a, h)] += ba[u]
        remote(g.at[u, rows(p.keep_a + (1 - p.bit_b) * q, q)], bm.at[u, pl.ds(0, q)], u, r2, p.dev_b)

    def stage2(u):
        p = Place(u)
        bytes_wait(bm.at[u, pl.ds(0, q)], send.at[u])
        grant(2, u, p.dev_b)
        bytes_wait(bm.at[u, pl.ds(0, q)], r2.at[u])
        g[u, rows(p.quarter, q)] += bm[u, pl.ds(0, q)]
        for d, to, dev in z_peers():
            remote(g.at[u, rows(p.quarter + to * e, e)], bm.at[u, pl.ds(q + (d - 1) * e, e)], u, r3, dev)

    def stage3(u):
        p = Place(u)
        bytes_wait(bm.at[u, pl.ds(q, 3 * e)], send.at[u])
        for _, _, dev in z_peers():
            grant(3, u, dev)
        bytes_wait(bm.at[u, pl.ds(q, 3 * e)], r3.at[u])
        left = rows(p.quarter + zc * e, e)
        g[u, left] = (g[u, left] + bm[u, pl.ds(q, e)]) + (bm[u, pl.ds(q + e, e)] + bm[u, pl.ds(q + 2 * e, e)])
        pl.semaphore_wait(credit.at[3, u], 3)
        for _, _, dev in z_peers():
            remote(g.at[u, left], g.at[u, left], u, r4, dev)

    def stage4(u):
        p = Place(u)
        bytes_wait(bm.at[u, pl.ds(q, 3 * e)], send.at[u])
        bytes_wait(bm.at[u, pl.ds(q, 3 * e)], r4.at[u])
        pl.semaphore_wait(credit.at[2, u], 1)
        block = rows(p.quarter, q)
        remote(g.at[u, block], g.at[u, block], u, r5, p.dev_b)

    def stage5(u):
        p = Place(u)
        bytes_wait(bm.at[u, pl.ds(0, q)], send.at[u])
        bytes_wait(bm.at[u, pl.ds(0, q)], r5.at[u])
        pl.semaphore_wait(credit.at[1, u], 1)
        block = rows(p.keep_a, h)
        remote(g.at[u, block], g.at[u, block], u, r6, p.dev_a)

    def stage6(u):
        bytes_wait(ba.at[u], send.at[u])
        bytes_wait(ba.at[u], r6.at[u])
        pl.semaphore_wait(credit.at[0, u], 1)
        remote(g.at[u, mine], g.at[u, mine], u, r7, partner)

    def stage7(u):
        bytes_wait(g.at[u, mine], send.at[u])
        bytes_wait(g.at[u, other], r7.at[u])
        is_fc = u < fc_units

        def out(ref, v, k):
            i, j = hbm_slice(v, 0)
            pltpu.make_async_copy(g.at[u], ref.at[rows((v // CS) * 2 * UR, 2 * UR), j], osem.at[k]).start()
        pl.when(is_fc)(lambda: out(of_ref, u, 0))
        pl.when(jnp.logical_not(is_fc))(lambda: out(oc_ref, u - fc_units, 1))
        kind = jnp.where(is_fc, 0, 1)
        limit = jnp.where(is_fc, fc_rows - (u // CS) * 2 * UR, 2 * UR)

        def square(k, c):
            x = g[u, rows(k * 8, 8)]
            return c + jnp.where(k * 8 < limit, x * x, 0.0)
        acc[kind] += lax.fori_loop(0, 2 * UR // 8, square, jnp.zeros((8, cols), F32))

    stages = (stage0, stage1, stage2, stage3, stage4, stage5, stage6, stage7)

    def step(t, c):
        for s in ORDER:
            u = t - DEPTH * s
            pl.when(jnp.logical_and(u >= 0, u < n_units))(functools.partial(stages[s], u))
        return c
    lax.fori_loop(0, n_units + DEPTH * (len(stages) - 1), step, 0)

    nrm_ref[...] = acc[...]
    bytes_wait(of_ref, osem.at[0])
    bytes_wait(oc_ref, osem.at[1])


def reduce_all(grad_fc, grad_conv, fc_rows, n_dev):
    width = grad_conv.shape[1]
    cols = width // CS
    fc_units = grad_fc.shape[0] // (2 * UR) * CS
    n_units = fc_units + grad_conv.shape[0] // (2 * UR) * CS
    dma = pltpu.SemaphoreType.DMA
    hbm = pl.BlockSpec(memory_space=pl.ANY)
    return pl.pallas_call(
        functools.partial(reduce_kernel, n_dev, fc_rows, fc_units, n_units),
        out_shape=(jax.ShapeDtypeStruct(grad_fc.shape, F32), jax.ShapeDtypeStruct(grad_conv.shape, F32),
                   jax.ShapeDtypeStruct((2, 8, cols), F32)),
        in_specs=[hbm, hbm],
        out_specs=(hbm, hbm, pl.BlockSpec(memory_space=pltpu.VMEM)),
        scratch_shapes=[
            pltpu.VMEM((n_units, 2 * UR, cols), F32),
            pltpu.VMEM((n_units, UR // 2, cols), F32),
            pltpu.VMEM((n_units, UR * 7 // 16, cols), F32),
            pltpu.VMEM((2, 8, cols), F32),
        ] + [dma((n_units,))] * 10 + [dma((2,)), pltpu.SemaphoreType.REGULAR((4, n_units))],
        compiler_params=pltpu.CompilerParams(collective_id=0, has_side_effects=True, vmem_limit_bytes=48 * 2 ** 20),
        name='reduce_all',
    )(grad_fc, grad_conv)


def solution(mesh):
    groups = mesh.shape['dp']

    def local_step(act_in, shortcut, labels, w_conv, bn_gamma, bn_beta, w_fc, fc_bias, vel_conv, vel_gamma, vel_beta, vel_fc, vel_bias, learn_rate):
        per_dev, side, _, c_mid = act_in.shape
        c_out = shortcut.shape[3]
        classes = w_fc.shape[1]
        spatial = side * side
        pos_count = per_dev * spatial
        global_rows = per_dev * groups
        act_grid = act_in.transpose(1, 2, 0, 3).reshape(spatial, per_dev, c_mid)
        short_grid = shortcut.transpose(1, 2, 0, 3).reshape(spatial, per_dev, c_out)
        conv_out = jnp.einsum('pbc,cd->pbd', act_grid, w_conv.astype(jnp.bfloat16), preferred_element_type=F32)
        batch_mean = jnp.mean(conv_out, axis=(0, 1))
        centered = conv_out - batch_mean
        inv_std = lax.rsqrt(jnp.mean(jnp.square(centered), axis=(0, 1)) + BN_EPS)
        x_hat = centered * inv_std
        pre_act = x_hat * bn_gamma + bn_beta + short_grid.astype(F32)
        pooled = jnp.mean(jax.nn.relu(pre_act), axis=0)
        pooled_bf = pooled.astype(jnp.bfloat16)
        fc_bf = w_fc.astype(jnp.bfloat16)
        logits = jnp.dot(pooled_bf, fc_bf, preferred_element_type=F32) + fc_bias
        log_prob = jax.nn.log_softmax(logits, axis=-1)
        one_hot_lab = (labels[:, None] == jnp.arange(classes, dtype=jnp.int32)[None, :]).astype(F32)
        target = SMOOTHING / classes + (1.0 - SMOOTHING) * one_hot_lab
        loss_part = -jnp.sum(target * log_prob) / global_rows
        d_logits = (jnp.exp(log_prob) - target) / global_rows
        d_bias = jnp.sum(d_logits, axis=0)
        d_logits_bf = d_logits.astype(jnp.bfloat16)
        d_pool = jnp.einsum('bk,ck->bc', d_logits_bf, fc_bf, preferred_element_type=F32) / spatial
        d_pre = jnp.where(pre_act > 0, d_pool[None], 0.0)
        d_beta = jnp.sum(d_pre, axis=(0, 1))
        d_gamma = jnp.sum(d_pre * x_hat, axis=(0, 1))
        d_conv_out = (bn_gamma * inv_std) * (d_pre - d_beta / pos_count - x_hat * (d_gamma / pos_count))
        d_conv = jnp.einsum('pbc,pbd->cd', act_grid, d_conv_out.astype(jnp.bfloat16), preferred_element_type=F32)

        padded = -(-classes // (2 * UR)) * 2 * UR
        d_fc = jnp.einsum('bk,bc->kc', jnp.pad(d_logits_bf, ((0, 0), (0, padded - classes))), pooled_bf, preferred_element_type=F32)
        last = jnp.concatenate([d_bias, loss_part[None], jnp.zeros((c_out - classes - 1,), F32)])
        small = jnp.concatenate([d_gamma[None], d_beta[None], last[None], jnp.zeros((5, c_out), F32)])
        d_fc = lax.dynamic_update_slice(d_fc, small, (classes, 0))

        g_fc, g_conv, sq = reduce_all(d_fc, d_conv, classes, groups)
        small = g_fc[classes:classes + 3]
        g_gamma, g_beta, g_bias, loss_val = small[0], small[1], small[2, :classes], small[2, classes]
        sq = jnp.sum(sq, axis=(1, 2))

        def lars(weight, gradient, velocity, g_sq):
            w_norm = jnp.sqrt(jnp.sum(jnp.square(weight)))
            trust = TRUST_COEF * w_norm / (jnp.sqrt(g_sq) + WEIGHT_DECAY * w_norm)
            new_vel = MOMENTUM * velocity + learn_rate * trust * (gradient + WEIGHT_DECAY * weight)
            return weight - new_vel, new_vel

        conv_new, conv_vel_new = lars(w_conv, g_conv, vel_conv, sq[1])
        fc_new, fc_vel_new = lars(w_fc.T, g_fc[:classes], vel_fc.T, sq[0])
        gamma_vel_new = MOMENTUM * vel_gamma + learn_rate * g_gamma
        beta_vel_new = MOMENTUM * vel_beta + learn_rate * g_beta
        bias_vel_new = MOMENTUM * vel_bias + learn_rate * g_bias
        return (conv_new, bn_gamma - gamma_vel_new, bn_beta - beta_vel_new, fc_new.T, fc_bias - bias_vel_new, conv_vel_new, gamma_vel_new, beta_vel_new, fc_vel_new.T, bias_vel_new, loss_val)

    return jax.shard_map(local_step, mesh=mesh, in_specs=(P('dp'),) * 3 + (P(),) * 11, out_specs=(P(),) * 11, check_vma=False)
```

time: 675 us -> 438 us (0.65)
  waiting for transfers between devices: 335 us -> 0 us
  Pallas kernels: 0 us -> 219 us
  local copies, waits for them, and re-layouts: 76 us -> 7.64 us
  blocking collectives: 42.6 us -> 0 us
  matrix products: 83.5 us -> 101 us
  other arithmetic: 118 us -> 104 us
  between operations: 18.3 us -> 4.97 us
    psum x1 -> x0, waiting for transfers between devices: 335 us -> none  [local_step(): lax.psum(local_terms, 'dp')]
    pallas_call x0 -> x1, Pallas kernels: none -> 219 us  [reduce_all(): pl.pallas_call(functools.partial(reduce_kernel, n_dev, fc_rows, fc_units,...]
    unnamed x24 -> x20, local copies, waits for them, and re-layouts: 76 us -> 5.64 us
    psum x1 -> x0, blocking collectives: 42.6 us -> none  [local_step(): lax.psum(local_terms, 'dp')]
    dot_general x5, matrix products: 83.5 us -> 101 us  [the longest x1 54.9 us: local_step(): jnp.einsum('pbc,pbd->cd', act_grid, d_conv_out.astype(jnp.bfloat16), pref...]
    reduce_sum x9 -> x8, other arithmetic: 74.8 us -> 58.4 us  [the longest x1 20.2 us: local_step(): d_gamma = jnp.sum(d_pre * x_hat, axis=(0, 1))]
    transpose x0 -> x1, other arithmetic: none -> 13.9 us  [local_step(): return (conv_new, bn_gamma - gamma_vel_new, bn_beta - beta_vel_new, fc_ne...]
    sub x2 -> x1, other arithmetic: 41.2 us -> 27.5 us  [lars(): return (weight - new_vel, new_vel)]
  transfers between devices with their start and end apart: 1 -> 0, of which waited for: 1 -> 0; matrix products, arithmetic and copies ran while one was open for 8% -> 0% of each run, Pallas kernels for 0% -> 0%
where the time goes in v1:
time: 438 us; the launch traced here: 437 us
  Pallas kernels  219 us (50%)
  other arithmetic  104 us (24%)
  matrix products  101 us (23%)
  local copies, waits for them, and re-layouts  7.64 us (2%)
  between operations  4.97 us (1%)
    pallas_call x1, Pallas kernels, reduce_all(): pl.pallas_call(functools.partial(reduce_kernel, n_dev, fc_rows, fc_units,...  219 us
    dot_general x1, matrix products, local_step(): jnp.einsum('pbc,pbd->cd', act_grid, d_conv_out.astype(jnp.bfloat16), pref...  54.9 us
    dot_general x1, matrix products, local_step(): jnp.einsum('pbc,cd->pbd', act_grid, w_conv.astype(jnp.bfloat16), preferre...  36.1 us
    sub x1, other arithmetic, lars(): return (weight - new_vel, new_vel)  27.5 us
    reduce_sum x1, other arithmetic, local_step(): d_gamma = jnp.sum(d_pre * x_hat, axis=(0, 1))  20.2 us
    reduce_sum x2, other arithmetic, lars(): w_norm = jnp.sqrt(jnp.sum(jnp.square(weight)))  16.7 us
    transpose x1, other arithmetic, local_step(): return (conv_new, bn_gamma - gamma_vel_new, bn_beta - beta_vel_new, fc_ne...  13.9 us
    reduce_sum x1, other arithmetic, local_step(): pooled = jnp.mean(jax.nn.relu(pre_act), axis=0)  10.3 us

profile of v1, /device:TPU:0, one launch (start us, length us, event | category | flops | bytes accessed | tf_op | source)
XLA Modules:
  0.0 437.5 jit_solution(6202320101042485431)
XLA Ops:
  0.6 36.1 %fusion.44 = (f32[2048]{0:T(1024)S(1)}, f32[49,64,2048]{2,1,0:T(8,128)}) fusion(bf16[49,64,2048]{2,1,0:T(8,128)(2,1)} %bitcast.70, f32[2048,2048]{1,0:T(8,128)} %param.17), kind=kOutput, calls=%fused_computation.71 | convolution fusion | flops 26317289472 | bytes 55320576 | tf_op jit(solution)/shard_map/pbc,cd->pbd/dot_general | solution.py:223
  36.8 10.0 %multiply_reduce_fusion = f32[2048]{0:T(1024)S(1)} fusion(f32[49,64,2048]{2,1,0:T(8,128)} %get-tuple-element.40, f32[2048]{0:T(1024)S(1)} %broadcast_multiply_fusion.2), kind=kLoop, calls=%fused_computation.9 | loop fusion | flops 19265536 | bytes 25706496 | tf_op jit(solution)/shard_map/reduce_sum | solution.py:226
  46.9 5.6 %copy-done = f32[49,64,2048]{2,1,0:T(8,128)S(1)} copy-done((f32[49,64,2048]{2,1,0:T(8,128)S(1)}, f32[49,64,2048]{2,1,0:T(8,128)}, u32[]{:S(2)}) %copy-start) | copy-done | bytes 25690136
  52.5 10.3 %maximum_reduce_fusion = f32[64,2048]{1,0:T(8,128)S(1)} fusion(f32[2048]{0:T(1024)S(1)} %copy-done.2, f32[2048]{0:T(1024)S(1)} %copy-done.1, f32[2048]{0:T(1024)S(1)} %get-tuple-element.36, f32[49,64,2048]{2,1,0:T(8,128)S(1)} %copy-done, f32[2048]{0:T(1024)S(1)} %broadcast_multiply_fusion.2, bf16[64,7,7,2048]{3,0,2,1:T(8,128)(2,1)} %param.15), kind=kLoop, calls=%fused_computation.8 | loop fusion | flops 51249152 | bytes 39092224 | tf_op jit(solution)/shard_map/reduce_sum | solution.py:229
  62.8 1.4 fusion.45
  64.3 0.2 exponential_reduce_fusion
  64.5 0.8 multiply_reduce_fusion.2
  65.3 4.7 %fusion.32 = f32[1024,2048]{1,0:T(8,128)} fusion(bf16[64,1000]{1,0:T(8,128)(2,1)S(1)} %get-tuple-element.34, f32[64,2048]{1,0:T(8,128)S(1)} %maximum_reduce_fusion), kind=kOutput, calls=%fused_computation.48 | convolution fusion | flops 268697600 | bytes 9040896 | tf_op jit(solution)/shard_map/bk,bc->kc/dot_general | solution.py:248
  70.8 4.3 convolution_multiply_fusion
  75.0 20.2 %fusion = (f32[2048]{0:T(1024)S(1)}, f32[2048]{0:T(1024)S(1)}, pred[49,64,2048]{2,1,0:T(32,128)(4,1)}) fusion(f32[49,64,2048]{2,1,0:T(8,128)} %get-tuple-element.40, f32[64,2048]{1,0:T(8,128)S(1)} %convolution_multiply_fusion, f32[2048]{0:T(1024)S(1)} %get-tuple-element.36, f32[2048]{0:T(1024)S(1)} %broadcast_multiply_fusion.2, ...), kind=kLoop, calls=%fused_computation.3 | loop fusion | flops 70643712 | bytes 45531136 | tf_op jit(solution)/shard_map/reduce_sum | solution.py:243
  95.3 0.7 maximum_dynamic-update-slice_fusion.gf_ref
  96.0 54.9 %fusion.13.gc_ref = f32[2048,2048]{1,0:T(8,128)} fusion(bf16[49,64,2048]{2,1,0:T(8,128)(2,1)} %bitcast.71, pred[49,64,2048]{2,1,0:T(32,128)(4,1)} %get-tuple-element.29, f32[49,64,2048]{2,1,0:T(8,128)} %get-tuple-element.40, f32[2048]{0:T(1024)S(1)} %get-tuple-element.43, f32[2048]{0:T(1024)S(1)} %get-tuple-element.44, f32[2048]{0:T(1024)S(1)} %get-tuple-element.35, ...), kind=kOutput, calls=%fused_computation.22 | convolution fusion | flops 26358054912 | bytes 62300160 | tf_op jit(solution)/shard_map/pbc,pbd->cd/dot_general | solution.py:245
  150.9 219.4 %reduce_all.1 = (f32[1024,2048]{1,0:T(8,128)}, f32[2048,2048]{1,0:T(8,128)}, f32[2,8,1024]{2,1,0:T(8,128)S(1)}) custom-call(f32[1024,2048]{1,0:T(8,128)} %maximum_dynamic-update-slice_fusion.gf_ref, f32[2048,2048]{1,0:T(8,128)} %fusion.13.gc_ref), custom_call_target="tpu_custom_call" | custom-call | tf_op jit(solution)/shard_map/reduce_all/pallas_call | solution.py:194
  371.0 10.7 %multiply_reduce_fusion.1 = f32[]{:T(128)} fusion(f32[2048,2048]{1,0:T(8,128)} %param.17), kind=kLoop, calls=%fused_computation.12 | loop fusion | flops 8388607 | bytes 16777220 | tf_op jit(solution)/shard_map/reduce_sum | solution.py:259
  382.5 0.6 fusion.43
  383.8 27.5 %fusion.42 = (f32[2048,2048]{1,0:T(8,128)}, f32[2048,2048]{1,0:T(8,128)}) fusion(f32[2048,2048]{1,0:T(8,128)} %param.17, f32[2048,2048]{1,0:T(8,128)} %get-tuple-element.15, f32[]{:T(128)S(6)} %mul.158, f32[2048,2048]{1,0:T(8,128)} %param.22), kind=kLoop, calls=%fused_computation.69 | loop fusion | flops 25165824 | bytes 83886080 | tf_op jit(solution)/shard_map/sub | solution.py:262
  411.3 0.9 slice_multiply_fusion
  412.2 0.6 fusion.41
  412.9 0.6 fusion.40
  413.5 6.0 %fusion.19 = f32[]{:T(128)} fusion(f32[2048,1000]{0,1:T(8,128)} %param.20), kind=kLoop, calls=%fused_computation.30 | loop fusion | flops 4095999 | bytes 8192004 | tf_op jit(solution)/shard_map/reduce_sum | solution.py:259
  420.9 13.9 %fusion.26 = (f32[2048,1000]{0,1:T(8,128)}, f32[2048,1000]{0,1:T(8,128)}) fusion(f32[2048,1000]{0,1:T(8,128)} %param.20, f32[1024,2048]{1,0:T(8,128)} %get-tuple-element.16, f32[]{:T(128)S(6)} %mul.175, f32[2048,1000]{0,1:T(8,128)} %param.25), kind=kLoop, calls=%fused_computation.38 | loop fusion | flops 12288000 | bytes 40960004 | tf_op jit(solution)/shard_map/transpose | solution.py:269
  434.8 0.8 slice_multiply_fusion.2
  435.6 0.6 fusion.39
  436.2 1.3 slice.32
  (29 shorter events, 0.3 us)
Async XLA Ops:
  36.8 10.1 %copy-start.1 = (f32[2048]{0:T(1024)S(1)}, f32[2048]{0:T(1024)}, u32[]{:S(2)}) copy-start(f32[2048]{0:T(1024)} %param.18) | copy-start | bytes 24580
  36.8 15.7 %copy-start = (f32[49,64,2048]{2,1,0:T(8,128)S(1)}, f32[49,64,2048]{2,1,0:T(8,128)}, u32[]{:S(2)}) copy-start(f32[49,64,2048]{2,1,0:T(8,128)} %get-tuple-element.40) | copy-start | bytes 77070336
  36.8 15.7 %copy-start.2 = (f32[2048]{0:T(1024)S(1)}, f32[2048]{0:T(1024)}, u32[]{:S(2)}) copy-start(f32[2048]{0:T(1024)} %param.19) | copy-start | bytes 24580
  36.8 26.0 %slice-start = ((s8[8192000]{0:T(1024)(128)(4,1)}), s8[4194304]{0:T(1024)(128)(4,1)S(1)}, s32[]{:S(2)}) async-start(s8[8192000]{0:T(1024)(128)(4,1)} %bitcast.62), calls=%async_computation | async-start | bytes 8388608
  52.5 10.3 %slice-start.1 = ((s8[8192000]{0:T(1024)(128)(4,1)}), s8[3997696]{0:T(1024)(128)(4,1)S(1)}, s32[]{:S(2)}) async-start(s8[8192000]{0:T(1024)(128)(4,1)} %bitcast.62), calls=%async_computation.1 | async-start | bytes 7995392
  52.5 10.3 %copy-start.3 = (f32[1000]{0:T(1024)S(1)}, f32[1000]{0:T(1024)}, u32[]{:S(2)}) copy-start(f32[1000]{0:T(1024)} %param.21) | copy-start | bytes 12004
  52.5 12.0 %copy-start.7 = (s32[64]{0:T(128)S(1)}, s32[64]{0:T(128)}, u32[]{:S(2)}) copy-start(s32[64]{0:T(128)} %param.16) | copy-start | bytes 772
  383.8 28.4 %copy-start.4 = (f32[2048]{0:T(1024)S(1)}, f32[2048]{0:T(1024)}, u32[]{:S(2)}) copy-start(f32[2048]{0:T(1024)} %param.23) | copy-start | bytes 24580
  383.8 29.1 %copy-start.5 = (f32[2048]{0:T(1024)S(1)}, f32[2048]{0:T(1024)}, u32[]{:S(2)}) copy-start(f32[2048]{0:T(1024)} %param.24) | copy-start | bytes 24580
  420.9 14.7 %copy-start.6 = (f32[1000]{0:T(1024)S(1)}, f32[1000]{0:T(1024)}, u32[]{:S(2)}) copy-start(f32[1000]{0:T(1024)} %param.26) | copy-start | bytes 12004

commit v2 on v1

--- a/solution.py
+++ b/solution.py
@@ -17,6 +17,9 @@
 UR = 128
 CS = 2
 DEPTH = 3
+SPOT_SLOTS = 4
+DOT_COLS = 256
+DB = 256
 ORDER = (3, 2, 1, 0, 7, 6, 5, 4)
 MESH_ID = pl.DeviceIdType.MESH
 
@@ -25,8 +28,9 @@
     pltpu.make_async_copy(ref, ref, sem).wait()
 
 
-def reduce_kernel(n_dev, fc_rows, fc_units, n_units, gf_ref, gc_ref, of_ref, oc_ref, nrm_ref,
-                  g, ba, bm, acc, ld, r0, r1, r2, r3, r4, r5, r6, r7, send, osem, credit):
+def reduce_kernel(n_dev, fc_rows, fc_units, n_units, gf_ref, a_ref, xh_ref, s_ref, gp_ref, vec_ref, of_ref, oc_ref, nrm_ref,
+                  g, ba, bm, acc, dz, abuf, stg, xbuf, sbuf,
+                  ld, r0, r1, r2, r3, r4, r5, r6, r7, send, osem, asem, xsem, ssem, credit):
     me = lax.axis_index('dp')
     core = me % 2
     zc = me // 8
@@ -85,16 +89,72 @@
             return c
         lax.fori_loop(first, last, step, 0)
 
+    spots, images = xh_ref.shape[0], xh_ref.shape[1]
+    pieces = fc_units - 1
+    per_piece = spots // pieces
+    assert per_piece * pieces == spots
+
+    def fetch_spot(p):
+        slot = p % SPOT_SLOTS
+        pltpu.make_async_copy(xh_ref.at[p], xbuf.at[slot], xsem.at[slot]).start()
+        pltpu.make_async_copy(s_ref.at[p], sbuf.at[slot], ssem.at[slot]).start()
+
+    def fetch_a(k):
+        for part, half in ((0, core), (1, 1 - core)):
+            pltpu.make_async_copy(a_ref.at[:, pl.ds(pl.multiple_of(k * 2 * UR + half * UR, 128), UR)],
+                                  abuf.at[k % 2, :, pl.ds(part * UR, UR)], asem.at[k % 2, part]).start()
+
+    for p in range(SPOT_SLOTS):
+        fetch_spot(p)
     load_from(gf_ref, 0, fc_units)
-    load_from(gc_ref, fc_units, n_units)
+    fetch_a(0)
+    fetch_a(1)
     acc[...] = jnp.zeros_like(acc)
     pl.semaphore_wait(barrier, n_dev - 1)
     pair_from(gf_ref, 0, fc_units)
-    pair_from(gc_ref, fc_units, n_units)
+
+    def spot_step(p, c):
+        slot = p % SPOT_SLOTS
+        bytes_wait(xbuf.at[slot], xsem.at[slot])
+        bytes_wait(sbuf.at[slot], ssem.at[slot])
+
+        def group(r, c):
+            x = xbuf[slot, pl.ds(pl.multiple_of(r * 16, 16), 16)]
+            pre = x * vec_ref[0:1] + vec_ref[1:2] + sbuf[slot, pl.ds(pl.multiple_of(r * 16, 16), 16)].astype(F32)
+            d = jnp.where(pre > 0, gp_ref[pl.ds(pl.multiple_of(r * 16, 16), 16)], 0.0) - vec_ref[2:3] - x * vec_ref[3:4]
+            dz[pl.ds(pl.multiple_of(p * images + r * 16, 16), 16)] = d.astype(jnp.bfloat16)
+            return c
+        lax.fori_loop(0, images // 16, group, 0)
+        pl.when(p + SPOT_SLOTS < spots)(lambda: fetch_spot(p + SPOT_SLOTS))
+        return c
+
+    def weight_grad(u):
+        v = u - fc_units
+        k = v // CS
+        cb = v % CS
+
+        @pl.when(cb == 0)
+        def _():
+            for part in range(2):
+                bytes_wait(abuf.at[k % 2, :, pl.ds(part * UR, UR)], asem.at[k % 2, part])
+
+        def block(n, c):
+            col = pl.multiple_of(n * DOT_COLS, 128)
+            out = lax.dot_general(abuf[k % 2], dz[:, pl.ds(pl.multiple_of(cb * cols + col, 128), DOT_COLS)],
+                                  (((0,), (0,)), ((), ())), preferred_element_type=F32)
+            g[u, mine, pl.ds(col, DOT_COLS)] = out[:UR]
+            stg[u % 4, :, pl.ds(col, DOT_COLS)] = out[UR:]
+            return c
+        lax.fori_loop(0, cols // DOT_COLS, block, 0)
+        remote(stg.at[u % 4], g.at[u, mine], u, r0, partner)
+
+        @pl.when(jnp.logical_and(cb == CS - 1, v + 1 + CS < n_units - fc_units))
+        def _():
+            fetch_a(k + 2)
 
     def stage0(u):
         p = Place(u)
-        bytes_wait(g.at[u, mine], ld.at[u])
+        pl.when(u < fc_units)(lambda: bytes_wait(g.at[u, mine], ld.at[u]))
         bytes_wait(g.at[u, mine], send.at[u])
         bytes_wait(g.at[u, other], r0.at[u])
         g[u, mine] += g[u, other]
@@ -176,6 +236,11 @@
         for s in ORDER:
             u = t - DEPTH * s
             pl.when(jnp.logical_and(u >= 0, u < n_units))(functools.partial(stages[s], u))
+
+        @pl.when(t < pieces)
+        def _():
+            lax.fori_loop(t * per_piece, (t + 1) * per_piece, spot_step, 0)
+        pl.when(jnp.logical_and(t >= pieces, t + 1 < n_units))(lambda: weight_grad(t + 1))
         return c
     lax.fori_loop(0, n_units + DEPTH * (len(stages) - 1), step, 0)
 
@@ -184,28 +249,215 @@
     bytes_wait(oc_ref, osem.at[1])
 
 
-def reduce_all(grad_fc, grad_conv, fc_rows, n_dev):
-    width = grad_conv.shape[1]
+def reduce_all(grad_fc, act, x_hat, short, gate, vec, fc_rows, n_dev):
+    rows_a, c_mid = act.shape
+    width = x_hat.shape[2]
     cols = width // CS
     fc_units = grad_fc.shape[0] // (2 * UR) * CS
-    n_units = fc_units + grad_conv.shape[0] // (2 * UR) * CS
+    n_units = fc_units + c_mid // (2 * UR) * CS
     dma = pltpu.SemaphoreType.DMA
     hbm = pl.BlockSpec(memory_space=pl.ANY)
+    vmem = pl.BlockSpec(memory_space=pltpu.VMEM)
+    bf16 = jnp.bfloat16
+    images = x_hat.shape[1]
     return pl.pallas_call(
         functools.partial(reduce_kernel, n_dev, fc_rows, fc_units, n_units),
-        out_shape=(jax.ShapeDtypeStruct(grad_fc.shape, F32), jax.ShapeDtypeStruct(grad_conv.shape, F32),
+        out_shape=(jax.ShapeDtypeStruct(grad_fc.shape, F32), jax.ShapeDtypeStruct((c_mid, width), F32),
                    jax.ShapeDtypeStruct((2, 8, cols), F32)),
-        in_specs=[hbm, hbm],
-        out_specs=(hbm, hbm, pl.BlockSpec(memory_space=pltpu.VMEM)),
+        in_specs=[hbm, hbm, hbm, hbm, vmem, vmem],
+        out_specs=(hbm, hbm, vmem),
         scratch_shapes=[
             pltpu.VMEM((n_units, 2 * UR, cols), F32),
             pltpu.VMEM((n_units, UR // 2, cols), F32),
             pltpu.VMEM((n_units, UR * 7 // 16, cols), F32),
             pltpu.VMEM((2, 8, cols), F32),
-        ] + [dma((n_units,))] * 10 + [dma((2,)), pltpu.SemaphoreType.REGULAR((4, n_units))],
-        compiler_params=pltpu.CompilerParams(collective_id=0, has_side_effects=True, vmem_limit_bytes=48 * 2 ** 20),
+            pltpu.VMEM((rows_a, width), bf16),
+            pltpu.VMEM((2, rows_a, 2 * UR), bf16),
+            pltpu.VMEM((4, UR, cols), F32),
+            pltpu.VMEM((SPOT_SLOTS, images, width), F32),
+            pltpu.VMEM((SPOT_SLOTS, images, width), bf16),
+        ] + [dma((n_units,))] * 10 + [dma((2,)), dma((2, 2)), dma((SPOT_SLOTS,)), dma((SPOT_SLOTS,)), pltpu.SemaphoreType.REGULAR((4, n_units))],
+        compiler_params=pltpu.CompilerParams(collective_id=0, has_side_effects=True, vmem_limit_bytes=67043328),
         name='reduce_all',
-    )(grad_fc, grad_conv)
+    )(grad_fc, act, x_hat, short, gate, vec)
+
+
+def forward_kernel(blocks, global_rows, a_ref, w_ref, s_ref, gb_ref, lab_ref, bias_ref, wfc_ref, xh_ref, dfc_ref, gate_ref, vec_ref, wsq_ref, fsq_ref,
+                   z0, z1, wb, stat, pool_s, cnt_s, sx_s, inv_s, big, fcb, sem):
+    j = pl.program_id(0)
+    spots, images, width = xh_ref.shape
+    total = spots * images
+    classes = wfc_ref.shape[0]
+    load_fc = pltpu.make_async_copy(wfc_ref, big.at[pl.ds(0, classes)], sem.at[0])
+
+    def run(now):
+        w = w_ref[...]
+        wb[...] = w.astype(jnp.bfloat16)
+        wsq_ref[...] = jnp.sum((w * w).reshape(w.shape[0] // 8, 8, width), axis=0)
+        out = jnp.dot(a_ref[...], wb[...], preferred_element_type=F32)
+        now[...] = out.reshape(spots, images, width)
+        mean = jnp.sum(out, axis=0, keepdims=True) / total
+        d = out - mean
+        var = jnp.sum(jnp.sum((d * d).reshape(total // 8, 8, width), axis=0), axis=0, keepdims=True) / total
+        stat[0:1] = mean
+        stat[1:2] = lax.rsqrt(var + BN_EPS)
+
+    def finish(z):
+        at = pl.ds(pl.multiple_of((j - 1) * width, 128), width)
+        mean, inv = mean_inv
+        gamma, beta = gb_ref[0:1, at], gb_ref[1:2, at]
+        inv_s[0:1, at] = inv
+        zero = jnp.zeros((8, width), F32)
+        for r in range(0, images, 8):
+            img = pl.ds(r, 8)
+            pool, cnt, sx = zero, zero, zero
+            for p in range(spots):
+                x = (z[p, img] - mean) * inv
+                xh_ref[p, img] = x
+                pre = x * gamma + beta + s_ref[p, img].astype(F32)
+                on = pre > 0
+                pool += jnp.where(on, pre, 0.0)
+                cnt += jnp.where(on, 1.0, 0.0)
+                sx += jnp.where(on, x, 0.0)
+            pool_s[img, at], cnt_s[img, at], sx_s[img, at] = pool, cnt, sx
+
+    mean_inv = stat[0:1], stat[1:2]
+    pl.when(j == 0)(load_fc.start)
+
+    @pl.when(j == 0)
+    def _():
+        run(z0)
+
+    @pl.when(jnp.logical_and(jnp.logical_and(j > 0, j < blocks), j % 2 == 0))
+    def _():
+        run(z0)
+        finish(z1)
+
+    @pl.when(jnp.logical_and(j < blocks, j % 2 == 1))
+    def _():
+        run(z1)
+        finish(z0)
+
+    @pl.when(j == blocks)
+    def _():
+        finish(z1 if blocks % 2 == 0 else z0)
+        load_fc.wait()
+        spread = gb_ref.shape[1]
+
+        def pack(i, c):
+            at = pl.ds(pl.multiple_of(i * 8, 8), 8)
+            w = big[at]
+            fcb[at] = w.astype(jnp.bfloat16)
+            return c + w * w
+        fsq_ref[...] = lax.fori_loop(0, classes // 8, pack, jnp.zeros((8, spread), F32))
+        pooled = (pool_s[...] / spots).astype(jnp.bfloat16)
+        wide = fcb[...]
+        logits = lax.dot_general(pooled, wide, (((1,), (1,)), ((), ())), preferred_element_type=F32) + bias_ref[...]
+        shifted = logits - jnp.max(logits, axis=1, keepdims=True)
+        log_prob = shifted - jnp.log(jnp.sum(jnp.exp(shifted), axis=1, keepdims=True))
+        hit = lab_ref[...] == lax.broadcasted_iota(jnp.int32, logits.shape, 1)
+        target = SMOOTHING / classes + (1.0 - SMOOTHING) * jnp.where(hit, 1.0, 0.0)
+        loss = -jnp.sum(target * log_prob) / global_rows
+        d_logits = (jnp.exp(log_prob) - target) / global_rows
+        d_bias = jnp.sum(d_logits, axis=0, keepdims=True)
+        d_bf = d_logits.astype(jnp.bfloat16)
+        big[pl.ds(0, classes)] = lax.dot_general(d_bf, pooled, (((0,), (0,)), ((), ())), preferred_element_type=F32)
+        d_pool = lax.dot_general(d_bf, wide, (((1,), (0,)), ((), ())), preferred_element_type=F32) / spots
+        d_beta = jnp.sum(d_pool * cnt_s[...], axis=0, keepdims=True)
+        d_gamma = jnp.sum(d_pool * sx_s[...], axis=0, keepdims=True)
+        gi = gb_ref[0:1] * inv_s[0:1]
+        gate_ref[...] = d_pool * gi
+        vec_ref[0:2] = gb_ref[0:2]
+        vec_ref[2:3] = gi * (d_beta / total)
+        vec_ref[3:4] = gi * (d_gamma / total)
+        rest = big.shape[0] - classes
+        big[pl.ds(classes, rest)] = jnp.zeros((rest, spread), F32)
+        big[pl.ds(classes, 1)] = d_gamma
+        big[pl.ds(classes + 1, 1)] = d_beta
+        big[pl.ds(classes + 2, 1), pl.ds(0, classes)] = d_bias
+        big[pl.ds(classes + 3, 1)] = jnp.full((1, spread), loss, F32)
+        store = pltpu.make_async_copy(big, dfc_ref, sem.at[1])
+        store.start()
+        store.wait()
+
+
+def forward(act, weight, short, scale, labels, bias, w_fct, global_rows):
+    rows_a, c_mid = act.shape
+    spots, images, c_out = short.shape
+    classes = w_fct.shape[0]
+    padded = -(-classes // (2 * UR)) * 2 * UR
+    blocks = c_out // DB
+    def now(j):
+        return 0, jnp.minimum(j, blocks - 1)
+    def late3(j):
+        return 0, 0, jnp.maximum(j - 1, 0)
+    def whole(shape):
+        return pl.BlockSpec(shape, lambda j: (0,) * len(shape), pipeline_mode=pl.Buffered(1))
+    hbm = pl.BlockSpec(memory_space=pl.ANY)
+    rows8 = jax.ShapeDtypeStruct((8, c_out), F32)
+    plane = pltpu.VMEM((images, c_out), F32)
+    return pl.pallas_call(
+        functools.partial(forward_kernel, blocks, global_rows),
+        grid=(blocks + 1,),
+        out_shape=(jax.ShapeDtypeStruct((spots, images, c_out), F32), jax.ShapeDtypeStruct((padded, c_out), F32),
+                   jax.ShapeDtypeStruct((images, c_out), F32), rows8, rows8, rows8),
+        in_specs=[whole((rows_a, c_mid)), pl.BlockSpec((c_mid, DB), now), pl.BlockSpec((spots, images, DB), late3),
+                  whole((8, c_out)), whole(labels.shape), whole(bias.shape), hbm],
+        out_specs=(pl.BlockSpec((spots, images, DB), late3), hbm, pl.BlockSpec((images, c_out), lambda j: (0, 0)),
+                   pl.BlockSpec((8, c_out), lambda j: (0, 0)), pl.BlockSpec((8, DB), now), pl.BlockSpec((8, c_out), lambda j: (0, 0))),
+        scratch_shapes=[pltpu.VMEM((spots, images, DB), F32)] * 2 + [pltpu.VMEM((c_mid, DB), jnp.bfloat16), pltpu.VMEM((8, DB), F32),
+                        plane, plane, plane, pltpu.VMEM((8, c_out), F32), pltpu.VMEM((padded, c_out), F32),
+                        pltpu.VMEM((classes, c_out), jnp.bfloat16), pltpu.SemaphoreType.DMA((2,))],
+        compiler_params=pltpu.CompilerParams(vmem_limit_bytes=63 * 2 ** 20),
+        name='forward',
+    )(act, weight, short, scale, labels, bias, w_fct)
+
+
+def update_kernel(conv_steps, lr_ref, nrm_ref, csq_ref, fsq_ref, gc_ref, wc_ref, vc_ref, gf_ref, wf_ref, vf_ref,
+                  wc_new, vc_new, wf_new, vf_new, rate):
+    i = pl.program_id(0)
+    lr = lr_ref[0, 0]
+
+    @pl.when(i == 0)
+    def _():
+        for k, sq_ref in ((0, csq_ref), (1, fsq_ref)):
+            w_norm = jnp.sqrt(jnp.sum(jnp.sum(sq_ref[...], axis=0, keepdims=True), axis=1, keepdims=True))
+            g_norm = jnp.sqrt(jnp.sum(jnp.sum(nrm_ref[1 - k], axis=0, keepdims=True), axis=1, keepdims=True))
+            rate[k:k + 1] = jnp.broadcast_to(lr * (TRUST_COEF * w_norm / (g_norm + WEIGHT_DECAY * w_norm)), (1, 128))
+
+    def apply(k, g_ref, w_ref, v_ref, w_out, v_out):
+        scale = rate[k:k + 1, 0:1]
+
+        def some(r, c):
+            at = pl.ds(pl.multiple_of(r * 8, 8), 8)
+            w = w_ref[at]
+            v = MOMENTUM * v_ref[at] + scale * (g_ref[at] + WEIGHT_DECAY * w)
+            v_out[at] = v
+            w_out[at] = w - v
+            return c
+        lax.fori_loop(0, w_ref.shape[0] // 8, some, 0, unroll=True)
+
+    pl.when(i < conv_steps)(lambda: apply(0, gc_ref, wc_ref, vc_ref, wc_new, vc_new))
+    pl.when(i >= conv_steps)(lambda: apply(1, gf_ref, wf_ref, vf_ref, wf_new, vf_new))
+
+
+def update(rate, norms, conv_sq, fc_sq, g_conv, w_conv, v_conv, g_fc, w_fct, v_fct):
+    width = w_conv.shape[1]
+    conv_rows, fc_rows = 256, 200
+    conv_steps, fc_steps = w_conv.shape[0] // conv_rows, w_fct.shape[0] // fc_rows
+    conv = pl.BlockSpec((conv_rows, width), lambda i: (jnp.minimum(i, conv_steps - 1), 0))
+    fc = pl.BlockSpec((fc_rows, width), lambda i: (jnp.maximum(i - conv_steps, 0), 0))
+    vmem = pl.BlockSpec(memory_space=pltpu.VMEM)
+    return pl.pallas_call(
+        functools.partial(update_kernel, conv_steps),
+        grid=(conv_steps + fc_steps,),
+        out_shape=(jax.ShapeDtypeStruct(w_conv.shape, F32),) * 2 + (jax.ShapeDtypeStruct(w_fct.shape, F32),) * 2,
+        in_specs=[pl.BlockSpec(memory_space=pltpu.SMEM), vmem, vmem, vmem, conv, conv, conv, fc, fc, fc],
+        out_specs=(conv, conv, fc, fc),
+        scratch_shapes=[pltpu.VMEM((8, 128), F32)],
+        compiler_params=pltpu.CompilerParams(vmem_limit_bytes=60 * 2 ** 20),
+        name='update',
+    )(rate, norms, conv_sq, fc_sq, g_conv, w_conv, v_conv, g_fc, w_fct, v_fct)
 
 
 def solution(mesh):
@@ -218,51 +470,15 @@
         spatial = side * side
         pos_count = per_dev * spatial
         global_rows = per_dev * groups
-        act_grid = act_in.transpose(1, 2, 0, 3).reshape(spatial, per_dev, c_mid)
-        short_grid = shortcut.transpose(1, 2, 0, 3).reshape(spatial, per_dev, c_out)
-        conv_out = jnp.einsum('pbc,cd->pbd', act_grid, w_conv.astype(jnp.bfloat16), preferred_element_type=F32)
-        batch_mean = jnp.mean(conv_out, axis=(0, 1))
-        centered = conv_out - batch_mean
-        inv_std = lax.rsqrt(jnp.mean(jnp.square(centered), axis=(0, 1)) + BN_EPS)
-        x_hat = centered * inv_std
-        pre_act = x_hat * bn_gamma + bn_beta + short_grid.astype(F32)
-        pooled = jnp.mean(jax.nn.relu(pre_act), axis=0)
-        pooled_bf = pooled.astype(jnp.bfloat16)
-        fc_bf = w_fc.astype(jnp.bfloat16)
-        logits = jnp.dot(pooled_bf, fc_bf, preferred_element_type=F32) + fc_bias
-        log_prob = jax.nn.log_softmax(logits, axis=-1)
-        one_hot_lab = (labels[:, None] == jnp.arange(classes, dtype=jnp.int32)[None, :]).astype(F32)
-        target = SMOOTHING / classes + (1.0 - SMOOTHING) * one_hot_lab
-        loss_part = -jnp.sum(target * log_prob) / global_rows
-        d_logits = (jnp.exp(log_prob) - target) / global_rows
-        d_bias = jnp.sum(d_logits, axis=0)
-        d_logits_bf = d_logits.astype(jnp.bfloat16)
-        d_pool = jnp.einsum('bk,ck->bc', d_logits_bf, fc_bf, preferred_element_type=F32) / spatial
-        d_pre = jnp.where(pre_act > 0, d_pool[None], 0.0)
-        d_beta = jnp.sum(d_pre, axis=(0, 1))
-        d_gamma = jnp.sum(d_pre * x_hat, axis=(0, 1))
-        d_conv_out = (bn_gamma * inv_std) * (d_pre - d_beta / pos_count - x_hat * (d_gamma / pos_count))
-        d_conv = jnp.einsum('pbc,pbd->cd', act_grid, d_conv_out.astype(jnp.bfloat16), preferred_element_type=F32)
-
-        padded = -(-classes // (2 * UR)) * 2 * UR
-        d_fc = jnp.einsum('bk,bc->kc', jnp.pad(d_logits_bf, ((0, 0), (0, padded - classes))), pooled_bf, preferred_element_type=F32)
-        last = jnp.concatenate([d_bias, loss_part[None], jnp.zeros((c_out - classes - 1,), F32)])
-        small = jnp.concatenate([d_gamma[None], d_beta[None], last[None], jnp.zeros((5, c_out), F32)])
-        d_fc = lax.dynamic_update_slice(d_fc, small, (classes, 0))
-
-        g_fc, g_conv, sq = reduce_all(d_fc, d_conv, classes, groups)
-        small = g_fc[classes:classes + 3]
-        g_gamma, g_beta, g_bias, loss_val = small[0], small[1], small[2, :classes], small[2, classes]
-        sq = jnp.sum(sq, axis=(1, 2))
-
-        def lars(weight, gradient, velocity, g_sq):
-            w_norm = jnp.sqrt(jnp.sum(jnp.square(weight)))
-            trust = TRUST_COEF * w_norm / (jnp.sqrt(g_sq) + WEIGHT_DECAY * w_norm)
-            new_vel = MOMENTUM * velocity + learn_rate * trust * (gradient + WEIGHT_DECAY * weight)
-            return weight - new_vel, new_vel
-
-        conv_new, conv_vel_new = lars(w_conv, g_conv, vel_conv, sq[1])
-        fc_new, fc_vel_new = lars(w_fc.T, g_fc[:classes], vel_fc.T, sq[0])
+        act = act_in.transpose(1, 2, 0, 3).reshape(pos_count, c_mid)
+        short = shortcut.transpose(1, 2, 0, 3).reshape(spatial, per_dev, c_out)
+        scale = jnp.concatenate([bn_gamma[None], bn_beta[None], jnp.zeros((6, c_out), F32)])
+        x_hat, d_fc, gate, vec, conv_sq, fc_sq = forward(act, w_conv, short, scale, labels[:, None], fc_bias[None], w_fc.T, global_rows)
+        g_fc, g_conv, norms = reduce_all(d_fc, act, x_hat, short, gate, vec, classes, groups)
+        small = g_fc[classes:classes + 4]
+        g_gamma, g_beta, g_bias, loss_val = small[0], small[1], small[2, :classes], small[3, 0]
+        conv_new, conv_vel_new, fc_new, fc_vel_new = update(learn_rate[None, None], norms, conv_sq, fc_sq, g_conv, w_conv, vel_conv,
+                                                            g_fc, w_fc.T, vel_fc.T)
         gamma_vel_new = MOMENTUM * vel_gamma + learn_rate * g_gamma
         beta_vel_new = MOMENTUM * vel_beta + learn_rate * g_beta
         bias_vel_new = MOMENTUM * vel_bias + learn_rate * g_bias

time: 438 us -> 333 us (0.76)
  Pallas kernels: 219 us -> 324 us
  matrix products: 101 us -> 0 us
  other arithmetic: 104 us -> 4.33 us
  local copies, waits for them, and re-layouts: 7.64 us -> 2.64 us
    dot_general x5 -> x0, matrix products: 101 us -> none  [the longest x1 54.9 us: local_step(): jnp.einsum('pbc,pbd->cd', act_grid, d_conv_out.astype(jnp.bfloat16), pref...]
    pallas_call x0 -> x2, Pallas kernels: none -> 101 us  [the longest x1 60.6 us: forward(): pl.pallas_call(functools.partial(forward_kernel, blocks, global_rows), gr...]
    reduce_sum x8 -> x0, other arithmetic: 58.4 us -> none  [the longest x1 20.2 us: local_step(): d_gamma = jnp.sum(d_pre * x_hat, axis=(0, 1))]
    sub x2 -> x0, other arithmetic: 28.1 us -> none  [the longest x1 27.5 us: lars(): return (weight - new_vel, new_vel)]
    transpose x1 -> x0, other arithmetic: 13.9 us -> none  [local_step(): return (conv_new, bn_gamma - gamma_vel_new, bn_beta - beta_vel_new, fc_ne...]
    unnamed x20 -> x12, local copies, waits for them, and re-layouts: 5.64 us -> 0.04 us
where the time goes in v2:
time: 333 us; the launch traced here: 332 us
  Pallas kernels  324 us (97%)
  other arithmetic  4.33 us (1%)
    pallas_call x1, Pallas kernels, reduce_all(): pl.pallas_call(functools.partial(reduce_kernel, n_dev, fc_rows, fc_units,...  222 us
    pallas_call x1, Pallas kernels, forward(): pl.pallas_call(functools.partial(forward_kernel, blocks, global_rows), gr...  60.6 us
    pallas_call x1, Pallas kernels, update(): pl.pallas_call(functools.partial(update_kernel, conv_steps), grid=(conv_s...  40.6 us

profile of v2, /device:TPU:0, one launch (start us, length us, event | category | flops | bytes accessed | tf_op | source)
XLA Modules:
  0.0 331.9 jit_solution(17432366227831966303)
XLA Ops:
  1.3 0.1 pad.2.clone
  1.4 1.4 maximum_maximum_fusion.gb_ref
  2.8 1.3 copy.25.lab_ref
  4.1 60.6 %forward.1 = (f32[49,64,2048]{2,1,0:T(8,128)}, f32[1024,2048]{1,0:T(8,128)}, f32[64,2048]{1,0:T(8,128)}, f32[8,2048]{1,0:T(8,128)}, f32[8,2048]{1,0:T(8,128)}, /*index=5*/f32[8,2048]{1,0:T(8,128)}) custom-call(bf16[3136,2048]{1,0:T(8,128)(2,1)} %bitcast.20, f32[2048,2048]{1,0:T(8,128)} %wc_ref.1, bf16[49,64,2048]{2,1,0:T(8,128)(2,1)} %bitcast.22, ...), custom_call_target="tpu_custom_call" | custom-call | tf_op jit(solution)/shard_map/forward/pallas_call | solution.py:399
  64.7 222.4 %reduce_all.1 = (f32[1024,2048]{1,0:T(8,128)}, f32[2048,2048]{1,0:T(8,128)}, f32[2,8,1024]{2,1,0:T(8,128)}) custom-call(f32[1024,2048]{1,0:T(8,128)} %get-tuple-element.24.gf_ref, bf16[3136,2048]{1,0:T(8,128)(2,1)} %bitcast.21, f32[49,64,2048]{2,1,0:T(8,128)} %get-tuple-element.25.xh_ref, bf16[49,64,2048]{2,1,0:T(8,128)(2,1)} %bitcast.23, ...), custom_call_target="tpu_custom_call" | custom-call | tf_op jit(solution)/shard_map/reduce_all/pallas_call | solution.py:263
  287.1 0.0 copy-start
  287.1 0.0 copy-start.1
  287.2 0.0 copy-start.3
  287.2 0.0 copy-start.4
  287.2 0.0 copy-start.2
  287.2 0.0 copy-start.5
  287.2 40.6 %update.1 = (f32[2048,2048]{1,0:T(8,128)}, f32[2048,2048]{1,0:T(8,128)}, f32[1000,2048]{1,0:T(8,128)}, f32[1000,2048]{1,0:T(8,128)}) custom-call(f32[1,1]{1,0:T(1,128)} %bitcast.19.lr_ref, f32[2,8,1024]{2,1,0:T(8,128)} %get-tuple-element.28.nrm_ref, f32[8,2048]{1,0:T(8,128)} %get-tuple-element.29.csq_ref, f32[8,2048]{1,0:T(8,128)} %get-tuple-element.30.fsq_ref, ...), custom_call_target="tpu_custom_call" | custom-call | tf_op jit(solution)/shard_map/update/pallas_call | solution.py:451
  327.8 0.9 slice_multiply_fusion
  328.7 0.0 copy-done
  328.7 0.0 copy-done.1
  328.7 0.0 copy-done.3
  328.8 0.0 copy-done.4
  328.8 0.6 fusion.1
  329.4 0.8 slice_multiply_fusion.2
  330.2 0.0 copy-done.2
  330.2 0.0 copy-done.5
  330.2 0.6 fusion
  330.8 1.2 slice.20
  (1 shorter events, 0.0 us)
Async XLA Ops:
  287.1 41.6 %copy-start = (f32[2048]{0:T(1024)S(1)}, f32[2048]{0:T(1024)}, u32[]{:S(2)}) copy-start(f32[2048]{0:T(1024)} %param.19) | copy-start | bytes 24580
  287.1 41.6 %copy-start.1 = (f32[2048]{0:T(1024)S(1)}, f32[2048]{0:T(1024)}, u32[]{:S(2)}) copy-start(f32[2048]{0:T(1024)} %param.18) | copy-start | bytes 24580
  287.2 41.6 %copy-start.3 = (f32[2048]{0:T(1024)S(1)}, f32[2048]{0:T(1024)}, u32[]{:S(2)}) copy-start(f32[2048]{0:T(1024)} %param.24) | copy-start | bytes 24580
  287.2 41.6 %copy-start.4 = (f32[2048]{0:T(1024)S(1)}, f32[2048]{0:T(1024)}, u32[]{:S(2)}) copy-start(f32[2048]{0:T(1024)} %param.23) | copy-start | bytes 24580
  287.2 43.0 %copy-start.2 = (f32[1000]{0:T(1024)S(1)}, f32[1000]{0:T(1024)}, u32[]{:S(2)}) copy-start(f32[1000]{0:T(1024)} %param.21) | copy-start | bytes 12004
  287.2 43.0 %copy-start.5 = (f32[1000]{0:T(1024)S(1)}, f32[1000]{0:T(1024)}, u32[]{:S(2)}) copy-start(f32[1000]{0:T(1024)} %param.26) | copy-start | bytes 12004

commit v3 on v2

--- a/solution.py
+++ b/solution.py
@@ -16,11 +16,12 @@
 F32 = jnp.float32
 UR = 128
 CS = 2
-DEPTH = 3
+OFFSETS = (0, 3, 5, 7, 9, 11, 13, 15, 18, 21)
 SPOT_SLOTS = 4
-DOT_COLS = 256
+DOT_COLS = 1024
 DB = 256
-ORDER = (3, 2, 1, 0, 7, 6, 5, 4)
+PIECES = 7
+LEVELS = 4
 MESH_ID = pl.DeviceIdType.MESH
 
 
@@ -30,40 +31,40 @@
 
 def reduce_kernel(n_dev, fc_rows, fc_units, n_units, gf_ref, a_ref, xh_ref, s_ref, gp_ref, vec_ref, of_ref, oc_ref, nrm_ref,
                   g, ba, bm, acc, dz, abuf, stg, xbuf, sbuf,
-                  ld, r0, r1, r2, r3, r4, r5, r6, r7, send, osem, asem, xsem, ssem, credit):
+                  ld, recv, send, osem, asem, xsem, ssem, credit):
     me = lax.axis_index('dp')
     core = me % 2
-    zc = me // 8
     partner = me + 1 - 2 * core
     cols = g.shape[2]
-    h, q, e = UR // 2, UR // 4, UR // 16
+    size = [UR >> i for i in range(LEVELS + 1)]
     mine = pl.ds(pl.multiple_of(core * UR, 8), UR)
     other = pl.ds(pl.multiple_of((1 - core) * UR, 8), UR)
 
     def rows(off, size):
         return pl.ds(pl.multiple_of(off, 8), size)
 
-    def remote(src, dst, u, sem, dev):
-        pltpu.make_async_remote_copy(src_ref=src, dst_ref=dst, send_sem=send.at[u], recv_sem=sem.at[u],
+    def remote(src, dst, u, k, dev):
+        pltpu.make_async_remote_copy(src_ref=src, dst_ref=dst, send_sem=send.at[u], recv_sem=recv.at[k, u],
                                      device_id=(dev,), device_id_type=MESH_ID).start()
 
     def grant(k, u, dev):
         pl.semaphore_signal(credit.at[k, u], inc=1, device_id=(dev,), device_id_type=MESH_ID)
 
-    class Place:
-        def __init__(self, u):
-            s_a = 2 + 2 * (u % 2)
-            s_b = 6 - s_a
-            bit_a = (me // s_a) % 2
-            self.bit_b = (me // s_b) % 2
-            self.dev_a = me + s_a * (1 - 2 * bit_a)
-            self.dev_b = me + s_b * (1 - 2 * self.bit_b)
-            self.keep_a = core * UR + bit_a * h
-            self.give_a = core * UR + (1 - bit_a) * h
-            self.quarter = self.keep_a + self.bit_b * q
-
-    def z_peers():
-        return [(d, (zc + d) % 4, (me + 8 * d) % n_dev) for d in (1, 3, 2)]
+    def levels(u):
+        s_a = 2 + 2 * (u % 2)
+        keep = core * UR
+        out = [(partner, keep, None)]
+        for i, stride in enumerate((s_a, 8, 6 - s_a, 16), 1):
+            bit = (me // stride) % 2
+            give = keep + (1 - bit) * size[i]
+            keep = keep + bit * size[i]
+            out.append((me + stride * (1 - 2 * bit), keep, give))
+        return out
+
+    def landing(u, i):
+        if i == 1:
+            return ba.at[u]
+        return bm.at[u, pl.ds(size[1] - size[i - 1], size[i])]
 
     barrier = pltpu.get_barrier_semaphore()
 
@@ -85,12 +86,12 @@
     def pair_from(ref, first, last):
         def step(u, c):
             i, j = hbm_slice(u - first, 1 - core)
-            remote(ref.at[i, j], g.at[u, mine], u, r0, partner)
+            remote(ref.at[i, j], g.at[u, mine], u, 0, partner)
             return c
         lax.fori_loop(first, last, step, 0)
 
     spots, images = xh_ref.shape[0], xh_ref.shape[1]
-    pieces = fc_units - 1
+    pieces = PIECES
     per_piece = spots // pieces
     assert per_piece * pieces == spots
 
@@ -146,75 +147,46 @@
             stg[u % 4, :, pl.ds(col, DOT_COLS)] = out[UR:]
             return c
         lax.fori_loop(0, cols // DOT_COLS, block, 0)
-        remote(stg.at[u % 4], g.at[u, mine], u, r0, partner)
+        remote(stg.at[u % 4], g.at[u, mine], u, 0, partner)
 
         @pl.when(jnp.logical_and(cb == CS - 1, v + 1 + CS < n_units - fc_units))
         def _():
             fetch_a(k + 2)
 
-    def stage0(u):
-        p = Place(u)
-        pl.when(u < fc_units)(lambda: bytes_wait(g.at[u, mine], ld.at[u]))
+    def reduce_stage(i, u):
+        at = levels(u)
+        dev, keep, _ = at[i]
+        if i == 0:
+            pl.when(u < fc_units)(lambda: bytes_wait(g.at[u, mine], ld.at[u]))
+            bytes_wait(g.at[u, mine], send.at[u])
+            bytes_wait(g.at[u, other], recv.at[0, u])
+            g[u, mine] += g[u, other]
+            grant(0, u, partner)
+        else:
+            bytes_wait(landing(u, i), send.at[u])
+            grant(i, u, dev)
+            bytes_wait(landing(u, i), recv.at[i, u])
+            g[u, rows(keep, size[i])] += landing(u, i)[...]
+        if i < LEVELS:
+            dev, _, give = at[i + 1]
+            remote(g.at[u, rows(give, size[i + 1])], landing(u, i + 1), u, i + 1, dev)
+        else:
+            gather_send(i, u, at)
+
+    def gather_send(i, u, at):
+        dev, keep, _ = at[i]
+        pl.semaphore_wait(credit.at[i, u], 1)
+        block = g.at[u, rows(keep, size[i])]
+        remote(block, block, u, 2 * LEVELS + 1 - i, dev)
+
+    def gather_stage(i, u):
+        bytes_wait(landing(u, i), send.at[u])
+        bytes_wait(landing(u, i), recv.at[2 * LEVELS + 1 - i, u])
+        gather_send(i - 1, u, levels(u))
+
+    def last_stage(u):
         bytes_wait(g.at[u, mine], send.at[u])
-        bytes_wait(g.at[u, other], r0.at[u])
-        g[u, mine] += g[u, other]
-        grant(0, u, partner)
-        remote(g.at[u, rows(p.give_a, h)], ba.at[u], u, r1, p.dev_a)
-
-    def stage1(u):
-        p = Place(u)
-        bytes_wait(ba.at[u], send.at[u])
-        grant(1, u, p.dev_a)
-        bytes_wait(ba.at[u], r1.at[u])
-        g[u, rows(p.keep_a, h)] += ba[u]
-        remote(g.at[u, rows(p.keep_a + (1 - p.bit_b) * q, q)], bm.at[u, pl.ds(0, q)], u, r2, p.dev_b)
-
-    def stage2(u):
-        p = Place(u)
-        bytes_wait(bm.at[u, pl.ds(0, q)], send.at[u])
-        grant(2, u, p.dev_b)
-        bytes_wait(bm.at[u, pl.ds(0, q)], r2.at[u])
-        g[u, rows(p.quarter, q)] += bm[u, pl.ds(0, q)]
-        for d, to, dev in z_peers():
-            remote(g.at[u, rows(p.quarter + to * e, e)], bm.at[u, pl.ds(q + (d - 1) * e, e)], u, r3, dev)
-
-    def stage3(u):
-        p = Place(u)
-        bytes_wait(bm.at[u, pl.ds(q, 3 * e)], send.at[u])
-        for _, _, dev in z_peers():
-            grant(3, u, dev)
-        bytes_wait(bm.at[u, pl.ds(q, 3 * e)], r3.at[u])
-        left = rows(p.quarter + zc * e, e)
-        g[u, left] = (g[u, left] + bm[u, pl.ds(q, e)]) + (bm[u, pl.ds(q + e, e)] + bm[u, pl.ds(q + 2 * e, e)])
-        pl.semaphore_wait(credit.at[3, u], 3)
-        for _, _, dev in z_peers():
-            remote(g.at[u, left], g.at[u, left], u, r4, dev)
-
-    def stage4(u):
-        p = Place(u)
-        bytes_wait(bm.at[u, pl.ds(q, 3 * e)], send.at[u])
-        bytes_wait(bm.at[u, pl.ds(q, 3 * e)], r4.at[u])
-        pl.semaphore_wait(credit.at[2, u], 1)
-        block = rows(p.quarter, q)
-        remote(g.at[u, block], g.at[u, block], u, r5, p.dev_b)
-
-    def stage5(u):
-        p = Place(u)
-        bytes_wait(bm.at[u, pl.ds(0, q)], send.at[u])
-        bytes_wait(bm.at[u, pl.ds(0, q)], r5.at[u])
-        pl.semaphore_wait(credit.at[1, u], 1)
-        block = rows(p.keep_a, h)
-        remote(g.at[u, block], g.at[u, block], u, r6, p.dev_a)
-
-    def stage6(u):
-        bytes_wait(ba.at[u], send.at[u])
-        bytes_wait(ba.at[u], r6.at[u])
-        pl.semaphore_wait(credit.at[0, u], 1)
-        remote(g.at[u, mine], g.at[u, mine], u, r7, partner)
-
-    def stage7(u):
-        bytes_wait(g.at[u, mine], send.at[u])
-        bytes_wait(g.at[u, other], r7.at[u])
+        bytes_wait(g.at[u, other], recv.at[2 * LEVELS + 1, u])
         is_fc = u < fc_units
 
         def out(ref, v, k):
@@ -230,19 +202,20 @@
             return c + jnp.where(k * 8 < limit, x * x, 0.0)
         acc[kind] += lax.fori_loop(0, 2 * UR // 8, square, jnp.zeros((8, cols), F32))
 
-    stages = (stage0, stage1, stage2, stage3, stage4, stage5, stage6, stage7)
+    stages = ([functools.partial(reduce_stage, i) for i in range(LEVELS + 1)]
+              + [functools.partial(gather_stage, i) for i in range(LEVELS, 0, -1)] + [last_stage])
 
     def step(t, c):
-        for s in ORDER:
-            u = t - DEPTH * s
+        for s in [*range(LEVELS, -1, -1), *range(2 * LEVELS + 1, LEVELS, -1)]:
+            u = t - OFFSETS[s]
             pl.when(jnp.logical_and(u >= 0, u < n_units))(functools.partial(stages[s], u))
 
         @pl.when(t < pieces)
         def _():
             lax.fori_loop(t * per_piece, (t + 1) * per_piece, spot_step, 0)
-        pl.when(jnp.logical_and(t >= pieces, t + 1 < n_units))(lambda: weight_grad(t + 1))
+        pl.when(jnp.logical_and(t + 1 >= fc_units, t + 1 < n_units))(lambda: weight_grad(t + 1))
         return c
-    lax.fori_loop(0, n_units + DEPTH * (len(stages) - 1), step, 0)
+    lax.fori_loop(0, n_units + OFFSETS[-1], step, 0)
 
     nrm_ref[...] = acc[...]
     bytes_wait(of_ref, osem.at[0])
@@ -276,13 +249,13 @@
             pltpu.VMEM((4, UR, cols), F32),
             pltpu.VMEM((SPOT_SLOTS, images, width), F32),
             pltpu.VMEM((SPOT_SLOTS, images, width), bf16),
-        ] + [dma((n_units,))] * 10 + [dma((2,)), dma((2, 2)), dma((SPOT_SLOTS,)), dma((SPOT_SLOTS,)), pltpu.SemaphoreType.REGULAR((4, n_units))],
+        ] + [dma((n_units,)), dma((2 * LEVELS + 2, n_units)), dma((n_units,)), dma((2,)), dma((2, 2)), dma((SPOT_SLOTS,)), dma((SPOT_SLOTS,)), pltpu.SemaphoreType.REGULAR((LEVELS + 1, n_units))],
         compiler_params=pltpu.CompilerParams(collective_id=0, has_side_effects=True, vmem_limit_bytes=67043328),
         name='reduce_all',
     )(grad_fc, act, x_hat, short, gate, vec)
 
 
-def forward_kernel(blocks, global_rows, a_ref, w_ref, s_ref, gb_ref, lab_ref, bias_ref, wfc_ref, xh_ref, dfc_ref, gate_ref, vec_ref, wsq_ref, fsq_ref,
+def forward_kernel(blocks, global_rows, a_ref, w_ref, s_ref, gamma_ref, beta_ref, lab_ref, bias_ref, wfc_ref, xh_ref, dfc_ref, gate_ref, vec_ref, wsq_ref, fsq_ref,
                    z0, z1, wb, stat, pool_s, cnt_s, sx_s, inv_s, big, fcb, sem):
     j = pl.program_id(0)
     spots, images, width = xh_ref.shape
@@ -305,7 +278,7 @@
     def finish(z):
         at = pl.ds(pl.multiple_of((j - 1) * width, 128), width)
         mean, inv = mean_inv
-        gamma, beta = gb_ref[0:1, at], gb_ref[1:2, at]
+        gamma, beta = gamma_ref[:, at], beta_ref[:, at]
         inv_s[0:1, at] = inv
         zero = jnp.zeros((8, width), F32)
         for r in range(0, images, 8):
@@ -342,7 +315,7 @@
     def _():
         finish(z1 if blocks % 2 == 0 else z0)
         load_fc.wait()
-        spread = gb_ref.shape[1]
+        spread = gamma_ref.shape[1]
 
         def pack(i, c):
             at = pl.ds(pl.multiple_of(i * 8, 8), 8)
@@ -355,7 +328,10 @@
         logits = lax.dot_general(pooled, wide, (((1,), (1,)), ((), ())), preferred_element_type=F32) + bias_ref[...]
         shifted = logits - jnp.max(logits, axis=1, keepdims=True)
         log_prob = shifted - jnp.log(jnp.sum(jnp.exp(shifted), axis=1, keepdims=True))
-        hit = lab_ref[...] == lax.broadcasted_iota(jnp.int32, logits.shape, 1)
+        square = (images, images)
+        own = lax.broadcasted_iota(jnp.int32, square, 0) == lax.broadcasted_iota(jnp.int32, square, 1)
+        labels = jnp.sum(jnp.where(own, lab_ref[...], 0), axis=1, keepdims=True)
+        hit = labels == lax.broadcasted_iota(jnp.int32, logits.shape, 1)
         target = SMOOTHING / classes + (1.0 - SMOOTHING) * jnp.where(hit, 1.0, 0.0)
         loss = -jnp.sum(target * log_prob) / global_rows
         d_logits = (jnp.exp(log_prob) - target) / global_rows
@@ -365,9 +341,10 @@
         d_pool = lax.dot_general(d_bf, wide, (((1,), (0,)), ((), ())), preferred_element_type=F32) / spots
         d_beta = jnp.sum(d_pool * cnt_s[...], axis=0, keepdims=True)
         d_gamma = jnp.sum(d_pool * sx_s[...], axis=0, keepdims=True)
-        gi = gb_ref[0:1] * inv_s[0:1]
+        gi = gamma_ref[...] * inv_s[0:1]
         gate_ref[...] = d_pool * gi
-        vec_ref[0:2] = gb_ref[0:2]
+        vec_ref[0:1] = gamma_ref[...]
+        vec_ref[1:2] = beta_ref[...]
         vec_ref[2:3] = gi * (d_beta / total)
         vec_ref[3:4] = gi * (d_gamma / total)
         rest = big.shape[0] - classes
@@ -381,7 +358,7 @@
         store.wait()
 
 
-def forward(act, weight, short, scale, labels, bias, w_fct, global_rows):
+def forward(act, weight, short, gamma, beta, labels, bias, w_fct, global_rows):
     rows_a, c_mid = act.shape
     spots, images, c_out = short.shape
     classes = w_fct.shape[0]
@@ -402,7 +379,7 @@
         out_shape=(jax.ShapeDtypeStruct((spots, images, c_out), F32), jax.ShapeDtypeStruct((padded, c_out), F32),
                    jax.ShapeDtypeStruct((images, c_out), F32), rows8, rows8, rows8),
         in_specs=[whole((rows_a, c_mid)), pl.BlockSpec((c_mid, DB), now), pl.BlockSpec((spots, images, DB), late3),
-                  whole((8, c_out)), whole(labels.shape), whole(bias.shape), hbm],
+                  whole(gamma.shape), whole(beta.shape), whole(labels.shape), whole(bias.shape), hbm],
         out_specs=(pl.BlockSpec((spots, images, DB), late3), hbm, pl.BlockSpec((images, c_out), lambda j: (0, 0)),
                    pl.BlockSpec((8, c_out), lambda j: (0, 0)), pl.BlockSpec((8, DB), now), pl.BlockSpec((8, c_out), lambda j: (0, 0))),
         scratch_shapes=[pltpu.VMEM((spots, images, DB), F32)] * 2 + [pltpu.VMEM((c_mid, DB), jnp.bfloat16), pltpu.VMEM((8, DB), F32),
@@ -410,11 +387,12 @@
                         pltpu.VMEM((classes, c_out), jnp.bfloat16), pltpu.SemaphoreType.DMA((2,))],
         compiler_params=pltpu.CompilerParams(vmem_limit_bytes=63 * 2 ** 20),
         name='forward',
-    )(act, weight, short, scale, labels, bias, w_fct)
+    )(act, weight, short, gamma, beta, labels, bias, w_fct)
 
 
 def update_kernel(conv_steps, lr_ref, nrm_ref, csq_ref, fsq_ref, gc_ref, wc_ref, vc_ref, gf_ref, wf_ref, vf_ref,
-                  wc_new, vc_new, wf_new, vf_new, rate):
+                  small_ref, *refs):
+    vectors, (wc_new, vc_new, wf_new, vf_new), vectors_new, (loss_ref, rate) = refs[:6], refs[6:10], refs[10:16], refs[16:]
     i = pl.program_id(0)
     lr = lr_ref[0, 0]
 
@@ -424,6 +402,13 @@
             w_norm = jnp.sqrt(jnp.sum(jnp.sum(sq_ref[...], axis=0, keepdims=True), axis=1, keepdims=True))
             g_norm = jnp.sqrt(jnp.sum(jnp.sum(nrm_ref[1 - k], axis=0, keepdims=True), axis=1, keepdims=True))
             rate[k:k + 1] = jnp.broadcast_to(lr * (TRUST_COEF * w_norm / (g_norm + WEIGHT_DECAY * w_norm)), (1, 128))
+
+        for k in range(3):
+            w_ref, v_ref = vectors[2 * k], vectors[2 * k + 1]
+            v = MOMENTUM * v_ref[...] + lr * small_ref[k:k + 1, 0:w_ref.shape[1]]
+            vectors_new[2 * k + 1][...] = v
+            vectors_new[2 * k][...] = w_ref[...] - v
+        loss_ref[...] = small_ref[3:4, 0:1]
 
     def apply(k, g_ref, w_ref, v_ref, w_out, v_out):
         scale = rate[k:k + 1, 0:1]
@@ -441,23 +426,25 @@
     pl.when(i >= conv_steps)(lambda: apply(1, gf_ref, wf_ref, vf_ref, wf_new, vf_new))
 
 
-def update(rate, norms, conv_sq, fc_sq, g_conv, w_conv, v_conv, g_fc, w_fct, v_fct):
+def update(rate, norms, conv_sq, fc_sq, g_conv, w_conv, v_conv, g_fc, w_fct, v_fct, vectors):
     width = w_conv.shape[1]
     conv_rows, fc_rows = 256, 200
     conv_steps, fc_steps = w_conv.shape[0] // conv_rows, w_fct.shape[0] // fc_rows
     conv = pl.BlockSpec((conv_rows, width), lambda i: (jnp.minimum(i, conv_steps - 1), 0))
     fc = pl.BlockSpec((fc_rows, width), lambda i: (jnp.maximum(i - conv_steps, 0), 0))
+    small = pl.BlockSpec((8, width), lambda i: (w_fct.shape[0] // 8, 0))
     vmem = pl.BlockSpec(memory_space=pltpu.VMEM)
     return pl.pallas_call(
         functools.partial(update_kernel, conv_steps),
         grid=(conv_steps + fc_steps,),
-        out_shape=(jax.ShapeDtypeStruct(w_conv.shape, F32),) * 2 + (jax.ShapeDtypeStruct(w_fct.shape, F32),) * 2,
-        in_specs=[pl.BlockSpec(memory_space=pltpu.SMEM), vmem, vmem, vmem, conv, conv, conv, fc, fc, fc],
-        out_specs=(conv, conv, fc, fc),
+        out_shape=(jax.ShapeDtypeStruct(w_conv.shape, F32),) * 2 + (jax.ShapeDtypeStruct(w_fct.shape, F32),) * 2
+        + tuple(jax.ShapeDtypeStruct(v.shape, F32) for v in vectors) + (jax.ShapeDtypeStruct((1, 1), F32),),
+        in_specs=[pl.BlockSpec(memory_space=pltpu.SMEM), vmem, vmem, vmem, conv, conv, conv, fc, fc, fc, small] + [vmem] * 6,
+        out_specs=(conv, conv, fc, fc) + (vmem,) * 7,
         scratch_shapes=[pltpu.VMEM((8, 128), F32)],
         compiler_params=pltpu.CompilerParams(vmem_limit_bytes=60 * 2 ** 20),
         name='update',
-    )(rate, norms, conv_sq, fc_sq, g_conv, w_conv, v_conv, g_fc, w_fct, v_fct)
+    )(rate, norms, conv_sq, fc_sq, g_conv, w_conv, v_conv, g_fc, w_fct, v_fct, g_fc, *vectors)
 
 
 def solution(mesh):
@@ -472,16 +459,11 @@
         global_rows = per_dev * groups
         act = act_in.transpose(1, 2, 0, 3).reshape(pos_count, c_mid)
         short = shortcut.transpose(1, 2, 0, 3).reshape(spatial, per_dev, c_out)
-        scale = jnp.concatenate([bn_gamma[None], bn_beta[None], jnp.zeros((6, c_out), F32)])
-        x_hat, d_fc, gate, vec, conv_sq, fc_sq = forward(act, w_conv, short, scale, labels[:, None], fc_bias[None], w_fc.T, global_rows)
+        x_hat, d_fc, gate, vec, conv_sq, fc_sq = forward(act, w_conv, short, bn_gamma[None], bn_beta[None], labels[None], fc_bias[None], w_fc.T, global_rows)
         g_fc, g_conv, norms = reduce_all(d_fc, act, x_hat, short, gate, vec, classes, groups)
-        small = g_fc[classes:classes + 4]
-        g_gamma, g_beta, g_bias, loss_val = small[0], small[1], small[2, :classes], small[3, 0]
-        conv_new, conv_vel_new, fc_new, fc_vel_new = update(learn_rate[None, None], norms, conv_sq, fc_sq, g_conv, w_conv, vel_conv,
-                                                            g_fc, w_fc.T, vel_fc.T)
-        gamma_vel_new = MOMENTUM * vel_gamma + learn_rate * g_gamma
-        beta_vel_new = MOMENTUM * vel_beta + learn_rate * g_beta
-        bias_vel_new = MOMENTUM * vel_bias + learn_rate * g_bias
-        return (conv_new, bn_gamma - gamma_vel_new, bn_beta - beta_vel_new, fc_new.T, fc_bias - bias_vel_new, conv_vel_new, gamma_vel_new, beta_vel_new, fc_vel_new.T, bias_vel_new, loss_val)
+        vectors = [v[None] for v in (bn_gamma, vel_gamma, bn_beta, vel_beta, fc_bias, vel_bias)]
+        new = update(learn_rate[None, None], norms, conv_sq, fc_sq, g_conv, w_conv, vel_conv, g_fc, w_fc.T, vel_fc.T, vectors)
+        conv_new, conv_vel, fc_new, fc_vel, gamma_new, gamma_vel, beta_new, beta_vel, bias_new, bias_vel, loss = new
+        return (conv_new, gamma_new[0], beta_new[0], fc_new.T, bias_new[0], conv_vel, gamma_vel[0], beta_vel[0], fc_vel.T, bias_vel[0], loss[0, 0])
 
     return jax.shard_map(local_step, mesh=mesh, in_specs=(P('dp'),) * 3 + (P(),) * 11, out_specs=(P(),) * 11, check_vma=False)

time: 333 us -> 305 us (0.916)
  Pallas kernels: 324 us -> 303 us
  other arithmetic: 4.33 us -> 0 us
    pallas_call x1, Pallas kernels: 222 us -> 202 us  [reduce_all(): pl.pallas_call(functools.partial(reduce_kernel, n_dev, fc_rows, fc_units,...]
where the time goes in v3:
time: 305 us
  Pallas kernels  303 us (99%)
    pallas_call x1, Pallas kernels, reduce_all(): pl.pallas_call(functools.partial(reduce_kernel, n_dev, fc_rows, fc_units,...  202 us
    pallas_call x1, Pallas kernels, forward(): pl.pallas_call(functools.partial(forward_kernel, blocks, global_rows), gr...  60.6 us
    pallas_call x1, Pallas kernels, update(): pl.pallas_call(functools.partial(update_kernel, conv_steps), grid=(conv_s...  40.8 us

profile of v3, /device:TPU:0, one launch (start us, length us, event | category | flops | bytes accessed | tf_op | source)
XLA Modules:
  0.0 304.8 jit_solution(10152957087912000598)
XLA Ops:
  1.3 60.6 %forward.1 = (f32[49,64,2048]{2,1,0:T(8,128)}, f32[1024,2048]{1,0:T(8,128)}, f32[64,2048]{1,0:T(8,128)}, f32[8,2048]{1,0:T(8,128)}, f32[8,2048]{1,0:T(8,128)}, /*index=5*/f32[8,2048]{1,0:T(8,128)}) custom-call(bf16[3136,2048]{1,0:T(8,128)(2,1)} %bitcast.26, f32[2048,2048]{1,0:T(8,128)} %wc_ref.1, bf16[49,64,2048]{2,1,0:T(8,128)(2,1)} %bitcast.28, ...), custom_call_target="tpu_custom_call" | custom-call | tf_op jit(solution)/shard_map/forward/pallas_call | solution.py:376
  61.9 202.0 %reduce_all.1 = (f32[1024,2048]{1,0:T(8,128)}, f32[2048,2048]{1,0:T(8,128)}, f32[2,8,1024]{2,1,0:T(8,128)}) custom-call(f32[1024,2048]{1,0:T(8,128)} %get-tuple-element.31.gf_ref, bf16[3136,2048]{1,0:T(8,128)(2,1)} %bitcast.27, f32[49,64,2048]{2,1,0:T(8,128)} %get-tuple-element.32.xh_ref, bf16[49,64,2048]{2,1,0:T(8,128)(2,1)} %bitcast.29, ...), custom_call_target="tpu_custom_call" | custom-call | tf_op jit(solution)/shard_map/reduce_all/pallas_call | solution.py:236
  263.8 40.8 %update.1 = (f32[2048,2048]{1,0:T(8,128)}, f32[2048,2048]{1,0:T(8,128)}, f32[1000,2048]{1,0:T(8,128)}, f32[1000,2048]{1,0:T(8,128)}, f32[1,2048]{1,0:T(1,128)}, ...) custom-call(f32[1,1]{1,0:T(1,128)} %bitcast.25.lr_ref, ...), custom_call_target="tpu_custom_call" | custom-call | tf_op jit(solution)/shard_map/update/pallas_call | solution.py:437

commit v4 on v3

--- a/solution.py
+++ b/solution.py
@@ -206,7 +206,7 @@
               + [functools.partial(gather_stage, i) for i in range(LEVELS, 0, -1)] + [last_stage])
 
     def step(t, c):
-        for s in [*range(LEVELS, -1, -1), *range(2 * LEVELS + 1, LEVELS, -1)]:
+        for s in [*range(2 * LEVELS + 1, LEVELS, -1), *range(LEVELS, -1, -1)]:
             u = t - OFFSETS[s]
             pl.when(jnp.logical_and(u >= 0, u < n_units))(functools.partial(stages[s], u))
 

time: 305 us -> 306 us (level)
  no operation moved by 1% of the time
where the time goes in v4:
time: 306 us; the launch traced here: 305 us
  Pallas kernels  304 us (99%)
    pallas_call x1, Pallas kernels, reduce_all(): pl.pallas_call(functools.partial(reduce_kernel, n_dev, fc_rows, fc_units,...  202 us
    pallas_call x1, Pallas kernels, forward(): pl.pallas_call(functools.partial(forward_kernel, blocks, global_rows), gr...  60.6 us
    pallas_call x1, Pallas kernels, update(): pl.pallas_call(functools.partial(update_kernel, conv_steps), grid=(conv_s...  40.8 us

profile of v4, /device:TPU:0, one launch (start us, length us, event | category | flops | bytes accessed | tf_op | source)
XLA Modules:
  0.0 305.2 jit_solution(4069672175239824398)
XLA Ops:
  1.3 60.6 %forward.1 = (f32[49,64,2048]{2,1,0:T(8,128)}, f32[1024,2048]{1,0:T(8,128)}, f32[64,2048]{1,0:T(8,128)}, f32[8,2048]{1,0:T(8,128)}, f32[8,2048]{1,0:T(8,128)}, /*index=5*/f32[8,2048]{1,0:T(8,128)}) custom-call(bf16[3136,2048]{1,0:T(8,128)(2,1)} %bitcast.26, f32[2048,2048]{1,0:T(8,128)} %wc_ref.1, bf16[49,64,2048]{2,1,0:T(8,128)(2,1)} %bitcast.28, ...), custom_call_target="tpu_custom_call" | custom-call | tf_op jit(solution)/shard_map/forward/pallas_call | solution.py:376
  61.9 202.4 %reduce_all.1 = (f32[1024,2048]{1,0:T(8,128)}, f32[2048,2048]{1,0:T(8,128)}, f32[2,8,1024]{2,1,0:T(8,128)}) custom-call(f32[1024,2048]{1,0:T(8,128)} %get-tuple-element.31.gf_ref, bf16[3136,2048]{1,0:T(8,128)(2,1)} %bitcast.27, f32[49,64,2048]{2,1,0:T(8,128)} %get-tuple-element.32.xh_ref, bf16[49,64,2048]{2,1,0:T(8,128)(2,1)} %bitcast.29, ...), custom_call_target="tpu_custom_call" | custom-call | tf_op jit(solution)/shard_map/reduce_all/pallas_call | solution.py:236
  264.3 40.8 %update.1 = (f32[2048,2048]{1,0:T(8,128)}, f32[2048,2048]{1,0:T(8,128)}, f32[1000,2048]{1,0:T(8,128)}, f32[1000,2048]{1,0:T(8,128)}, f32[1,2048]{1,0:T(1,128)}, ...) custom-call(f32[1,1]{1,0:T(1,128)} %bitcast.25.lr_ref, ...), custom_call_target="tpu_custom_call" | custom-call | tf_op jit(solution)/shard_map/update/pallas_call | solution.py:437
